TPU v7x, 256 devices: a whole 4x4x8 slice. The times are simulated.
256 devices in a mesh: region: 32 (over x, z), member: 8 (over y, core).
Axes of the slice: x: 4, y: 4, z: 8, core: 2. Of those that a mesh axis runs over, the one named last changes fastest.
Arguments:
- ensemble: bfloat16 [80, 524288], P('member', 'region'), may hold values from -6 to 6
- obs_value: float32 [8192, 128], P(('region', 'member')), may hold values from -8 to 8
- obs_var: float32 [8192, 128], P(('region', 'member')), may hold values from 0.1 to 1
- obs_point: int32 [8192, 128], P(('region', 'member')), may hold values from 0 to 16383
- owned_blocks: int32 [4096], P('region'), may hold values from 0 to 4095, each once
- infl_mean: float32 [4096], replicated, may hold values from 0.6 to 1.6
- infl_var: float32 [4096], replicated, may hold values from 0.0001 to 0.1
Outputs:
- inflated: bfloat16 [80, 524288], P('member', 'region')
- infl_post: float32 [4096], P(('region', 'member'))
Inputs may be any that keep to these rules, and one draw needn't show every extreme that they name: `obs_point`: index among the 16384 points of the observation's region; the observation belongs to the block of that point's slot. `owned_blocks`: every block id appears exactly once.
All inputs are finite; a program needn't handle non-finite values.
Results may differ from a plain program's by a relative error of at most 0.001.
Values sent between devices are 32-bit elements; how exact they have to be, the bound alone decides.
A program may use at most 64 MiB of HBM per device.

v0:
```python
import jax
import jax.numpy as jnp
from jax import lax
from jax.sharding import PartitionSpec as P


def sent_to_all(shard, axis):
    count = lax.axis_size(axis)
    return lax.all_to_all(
        jnp.broadcast_to(shard[None], (count, *shard.shape)), axis, 0, 0, tiled=True
    )


def over_copies(shard, axis):
    return sent_to_all(shard, axis).sum(axis=0)


def together(arrays, axis):
    line, at, gathered = (jnp.concatenate([a.reshape(-1) for a in arrays]), 0, [])
    total = over_copies(line, axis)
    for a in arrays:
        gathered.append(total[at : at + a.size].reshape(a.shape))
        at += a.size
    return tuple(gathered)


def split_up(shard, dim, count):
    shape = shard.shape
    parts = shard.reshape(*shape[:dim], count, shape[dim] // count, *shape[dim + 1 :])
    return jnp.moveaxis(parts, dim, 0)


def sum_at_owner(shard, axis, dim):
    parts = split_up(shard, dim, lax.axis_size(axis))
    arrived = lax.all_to_all(parts, axis, split_axis=0, concat_axis=0, tiled=True)
    return arrived.sum(axis=0)


def posterior(sums, prior_mean, prior_var):
    innov_sum = sums[0]
    spread_sum = sums[1]
    error_sum = sums[2]
    spread_spread = sums[3]
    spread_error = sums[4]
    error_error = sums[5]
    weight_var = (
        2.0 * prior_mean * prior_mean * (1.0 + spread_spread)
        + 4.0 * prior_mean * spread_error
        + 2.0 * error_error
    )
    value = (prior_mean * weight_var + prior_var * spread_sum * (innov_sum - error_sum)) / (
        weight_var + prior_var * spread_sum * spread_sum
    )
    return jnp.maximum(value, 1.0)


def bin_slots(innovation, spread, errors, slot_of, slots):
    count = innovation.shape[0]
    width = min(count, 2048)
    while count % width != 0:
        width = width // 2
    blocks = count // width
    inno = innovation.reshape(blocks, width)
    sprd = spread.reshape(blocks, width)
    errs = errors.reshape(blocks, width)
    columns = jnp.stack([inno * inno, sprd, errs, sprd * sprd, sprd * errs, errs * errs], 1)
    labels = slot_of.reshape(blocks, width)
    slot_ids = jnp.arange(slots, dtype=jnp.int32)

    def one_block(carry, pair):
        block_cols, block_labels = pair
        onehot = (block_labels[:, None] == slot_ids[None, :]).astype(jnp.float32)
        return (
            carry
            + jnp.dot(
                block_cols,
                onehot,
                precision=lax.Precision.HIGHEST,
                preferred_element_type=jnp.float32,
            ),
            None,
        )

    total, unused = lax.scan(one_block, jnp.zeros((6, slots), jnp.float32), (columns, labels))
    return total


def body(ensemble, obs_value, obs_var, obs_point, owned_blocks, infl_mean, infl_var):
    members = ensemble.shape[0] * lax.axis_size("member")
    wide = ensemble.astype(jnp.float32)
    local_total = jnp.sum(wide, 0)
    local_square = jnp.sum(wide * wide, 0)
    own_points = obs_point.reshape(-1)
    point_total, point_square = together((local_total, local_square), "member")
    point_mean = point_total / members
    at_square = point_square[own_points]
    at_mean = point_mean[own_points]
    spread = (at_square - members * at_mean * at_mean) / (members - 1)
    innovation = obs_value.reshape(-1) - at_mean
    errors = obs_var.reshape(-1)
    slots = owned_blocks.shape[0]
    span = point_mean.shape[0] // slots
    slot_of = own_points // span
    slot_sums = bin_slots(innovation, spread, errors, slot_of, slots)
    num_blocks = infl_mean.shape[0]
    share = num_blocks // lax.axis_size(("region", "member"))
    totals = over_copies(slot_sums, "member")
    lambda_owned = posterior(totals, infl_mean[owned_blocks], infl_var[owned_blocks])
    placed_lambda = jnp.zeros((num_blocks,), jnp.float32).at[owned_blocks].set(lambda_owned)
    region_part = sum_at_owner(placed_lambda, "region", 0)
    lambda_mine = lax.dynamic_slice_in_dim(region_part, lax.axis_index("member") * share, share)
    factor = jnp.sqrt(lambda_owned)[None, :, None]
    mean_slots = point_mean.reshape(1, slots, -1)
    shaped = wide.reshape(wide.shape[0], slots, -1)
    inflated = (
        (mean_slots + factor * (shaped - mean_slots)).astype(jnp.bfloat16).reshape(ensemble.shape)
    )
    return (inflated, lambda_mine)


def solution(mesh):
    placed = (
        P("member", "region"),
        P(("region", "member"), None),
        P(("region", "member"), None),
        P(("region", "member"), None),
        P("region"),
        P(),
        P(),
    )
    return jax.shard_map(
        body,
        mesh=mesh,
        in_specs=placed,
        out_specs=(P("member", "region"), P(("region", "member"))),
        check_vma=False,
    )
```

profile of v0, /device:TPU:1, one launch (start us, length us, event | category | flops | bytes accessed | tf_op | source)
XLA Modules:
  0.0 104.7 jit_solution(8019480347606360561)
XLA Ops:
  0.6 0.0 copy-start
  0.6 1.5 %convert_reduce_fusion = (f32[16384]{0:T(1024)S(1)}, f32[16384]{0:T(1024)S(1)}) fusion(bf16[10,16384]{1,0:T(8,128)(2,1)} %param.9), kind=kLoop, calls=%fused_computation.15 | loop fusion | flops 622592 | bytes 458752 | tf_op jit(solution)/shard_map/reduce_sum | solution.py:91
  2.1 1.5 %broadcast_in_dim.12 = f32[8,1,32768]{2,1,0:T(1,128)} broadcast(f32[32768]{0:T(1024)S(1)} %pad_maximum_fusion), dimensions={2} | broadcast | bytes 1179648 | tf_op jit(solution)/shard_map/broadcast_in_dim | solution.py:10
  3.6 0.0 copy-start.4
  3.6 6.8 %all-to-all-start = ((f32[8,1,32768]{2,1,0:T(1,128)}), f32[8,1,32768]{2,1,0:T(1,128)S(1)}, u32[]{:S(2)}, u32[]{:S(2)}) async-start(f32[8,1,32768]{2,1,0:T(1,128)} %broadcast_in_dim.12), calls=%async_computation | async-start | bytes 2097152 | tf_op jit(solution)/shard_map/all_to_all | solution.py:9
  10.4 0.0 copy-done.4
  10.5 0.0 copy-start.6
  10.5 0.6 copy-done.6
  11.2 14.2 %all-to-all-done = f32[8,1,32768]{2,1,0:T(1,128)S(1)} async-done(((f32[8,1,32768]{2,1,0:T(1,128)}), f32[8,1,32768]{2,1,0:T(1,128)S(1)}, u32[]{:S(2)}, u32[]{:S(2)}) %all-to-all-start) | async-done | bytes 1048608 | tf_op jit(solution)/shard_map/all_to_all | solution.py:9
  25.4 0.8 reduce_sum.47
  26.2 23.0 %gather_fusion.1 = f32[4096]{0:T(1024)S(1)} fusion(f32[16384]{0:T(1024)S(1)} %get-tuple-element.62, s32[4096]{0:T(1024)S(1)} %broadcast_clamp_fusion), kind=kCustom, calls=%fused_computation.1 | custom fusion | bytes 49152 | tf_op jit(solution)/shard_map/gather | solution.py:97
  49.3 0.0 copy-start.3
  49.3 0.0 copy-start.5
  49.3 23.0 %gather_fusion.2 = f32[4096]{0:T(1024)S(1)} fusion(f32[16384]{0:T(1024)S(1)} %get-tuple-element.61, s32[4096]{0:T(1024)S(1)} %broadcast_clamp_fusion), kind=kCustom, calls=%fused_computation.2 | custom fusion | bytes 49152 | tf_op jit(solution)/shard_map/gather | solution.py:96
  72.3 0.0 copy-done.3
  72.3 0.0 copy-done.5
  72.3 0.1 fusion.22
  72.4 0.2 stack.2
  72.6 1.2 %while.11 = (s32[]{:T(128)}, f32[6,128]{1,0:T(8,128)S(1)}, f32[2,6,2048]{2,1,0:T(8,128)S(1)}, s32[2,2048]{1,0:T(2,128)S(1)}, s32[]{:T(128)}, /*index=5*/s32[]{:T(128)}) while((s32[]{:T(128)}, f32[6,128]{1,0:T(8,128)S(1)}, f32[2,6,2048]{2,1,0:T(8,128)S(1)}, s32[2,2048]{1,0:T(2,128)S(1)}, s32[]{:T(128)}, /*index=5*/s32[]{:T(128)}) %tuple.32), condition=%wide.region_4.5_spmd.clone, body=%wide.region_3.4_spmd.clone.sunk | while | flops 19138052 | bytes 97367 | solution.py:84
  72.6 0.6 convolution_add_fusion.2
  73.2 0.6 convolution_add_fusion.2
  73.8 0.6 broadcast_in_dim.15
  74.5 4.2 %all-to-all-start.1 = ((f32[8,6,128]{2,1,0:T(8,128)}), f32[8,6,128]{2,1,0:T(8,128)S(1)}, u32[]{:S(2)}, u32[]{:S(2)}) async-start(f32[8,6,128]{2,1,0:T(8,128)} %broadcast_in_dim.15), calls=%async_computation.1 | async-start | bytes 65536 | tf_op jit(solution)/shard_map/all_to_all | solution.py:9
  78.7 0.0 copy-done
  78.7 0.0 copy-start.1
  78.7 0.0 copy-start.2
  78.7 1.1 %gather_fusion = f32[128]{0:T(128)S(1)} fusion(f32[4096]{0:T(1024)S(1)} %copy-done, s32[1024]{0:T(1024)S(1)} %pad_clamp_fusion), kind=kCustom, calls=%fused_computation | custom fusion | bytes 1536 | tf_op jit(solution)/shard_map/gather | solution.py:108
  79.9 0.0 copy-done.1
  79.9 1.1 %gather_fusion.3 = f32[128]{0:T(128)S(1)} fusion(f32[4096]{0:T(1024)S(1)} %copy-done.1, s32[1024]{0:T(1024)S(1)} %pad_clamp_fusion), kind=kCustom, calls=%fused_computation.3 | custom fusion | bytes 1536 | tf_op jit(solution)/shard_map/gather | solution.py:108
  81.1 2.4 %all-to-all-done.1 = f32[8,6,128]{2,1,0:T(8,128)S(1)} async-done(((f32[8,6,128]{2,1,0:T(8,128)}), f32[8,6,128]{2,1,0:T(8,128)S(1)}, u32[]{:S(2)}, u32[]{:S(2)}) %all-to-all-start.1) | async-done | bytes 24608 | tf_op jit(solution)/shard_map/all_to_all | solution.py:9
  83.5 0.1 broadcast_bitcast_fusion
  83.5 1.6 %scatter_custom_fusion = f32[4096]{0:T(1024)} fusion(s32[128]{0:T(128)S(1)} %compare_select_fusion.1, f32[128]{0:T(128)S(1)} %get-tuple-element.58, f32[]{:T(128)} %constant.23.clone.1), kind=kCustom, calls=%fused_computation.33 | custom fusion | bytes 16388 | tf_op jit(solution)/shard_map/scatter | solution.py:109
  85.1 10.3 %all-to-all-start.2 = ((f32[32,1,128]{2,1,0:T(1,128)}), f32[32,1,128]{2,1,0:T(1,128)S(1)}, u32[]{:S(2)}, u32[]{:S(2)}) async-start(f32[32,1,128]{2,1,0:T(1,128)} %bitcast.12), calls=%async_computation.2 | async-start | bytes 32768 | tf_op jit(solution)/shard_map/all_to_all | solution.py:35
  95.4 0.0 copy-done.2
  95.4 0.9 fusion.9
  96.4 7.7 %all-to-all-done.2 = f32[32,1,128]{2,1,0:T(1,128)S(1)} async-done(((f32[32,1,128]{2,1,0:T(1,128)}), f32[32,1,128]{2,1,0:T(1,128)S(1)}, u32[]{:S(2)}, u32[]{:S(2)}) %all-to-all-start.2) | async-done | bytes 16416 | tf_op jit(solution)/shard_map/all_to_all | solution.py:35
  104.1 0.6 dynamic_slice.11
  (15 shorter events, 0.2 us)
Async XLA Ops:
  0.6 78.1 %copy-start = (f32[4096]{0:T(1024)S(1)}, f32[4096]{0:T(1024)}, u32[]{:S(2)}) copy-start(f32[4096]{0:T(1024)} %param.14) | copy-start | bytes 49156
  3.6 6.8 %copy-start.4 = (s32[32,128]{1,0:T(8,128)S(1)}, s32[32,128]{1,0:T(8,128)}, u32[]{:S(2)}) copy-start(s32[32,128]{1,0:T(8,128)} %param.12) | copy-start | bytes 49156
  3.6 21.8 %all-to-all-start = ((f32[8,1,32768]{2,1,0:T(1,128)}), f32[8,1,32768]{2,1,0:T(1,128)S(1)}, u32[]{:S(2)}, u32[]{:S(2)}) async-start(f32[8,1,32768]{2,1,0:T(1,128)} %broadcast_in_dim.12), calls=%async_computation | async-start | bytes 2097152 | tf_op jit(solution)/shard_map/all_to_all | solution.py:9
  10.5 0.7 copy-start.6
  49.3 23.1 %copy-start.3 = (f32[32,128]{1,0:T(8,128)S(1)}, f32[32,128]{1,0:T(8,128)}, u32[]{:S(2)}) copy-start(f32[32,128]{1,0:T(8,128)} %param.11) | copy-start | bytes 49156
  49.3 23.1 %copy-start.5 = (f32[32,128]{1,0:T(8,128)S(1)}, f32[32,128]{1,0:T(8,128)}, u32[]{:S(2)}) copy-start(f32[32,128]{1,0:T(8,128)} %param.10) | copy-start | bytes 49156
  74.5 8.9 %all-to-all-start.1 = ((f32[8,6,128]{2,1,0:T(8,128)}), f32[8,6,128]{2,1,0:T(8,128)S(1)}, u32[]{:S(2)}, u32[]{:S(2)}) async-start(f32[8,6,128]{2,1,0:T(8,128)} %broadcast_in_dim.15), calls=%async_computation.1 | async-start | bytes 65536 | tf_op jit(solution)/shard_map/all_to_all | solution.py:9
  78.7 1.2 %copy-start.1 = (f32[4096]{0:T(1024)S(1)}, f32[4096]{0:T(1024)}, u32[]{:S(2)}) copy-start(f32[4096]{0:T(1024)} %param.15) | copy-start | bytes 49156
  78.7 16.7 %copy-start.2 = (bf16[10,16384]{1,0:T(8,128)(2,1)S(1)}, bf16[10,16384]{1,0:T(8,128)(2,1)}, u32[]{:S(2)}) copy-start(bf16[10,16384]{1,0:T(8,128)(2,1)} %param.9) | copy-start | bytes 983044
  85.1 19.0 %all-to-all-start.2 = ((f32[32,1,128]{2,1,0:T(1,128)}), f32[32,1,128]{2,1,0:T(1,128)S(1)}, u32[]{:S(2)}, u32[]{:S(2)}) async-start(f32[32,1,128]{2,1,0:T(1,128)} %bitcast.12), calls=%async_computation.2 | async-start | bytes 32768 | tf_op jit(solution)/shard_map/all_to_all | solution.py:35
where the time goes:
time: 105 us
  local copies, waits for them, and re-layouts  53.6 us (51%)
  waiting for transfers between devices  24.3 us (23%)
  starting transfers between devices  21.3 us (20%)
  other arithmetic  3.4 us (3%)
  matrix products  1.15 us (1%)
    gather x1, local copies, waits for them, and re-layouts, body(): at_mean = point_mean[own_points]  23 us
    gather x1, local copies, waits for them, and re-layouts, body(): at_square = point_square[own_points]  23 us
    all_to_all x2, waiting for transfers between devices, sent_to_all(): lax.all_to_all(jnp.broadcast_to(shard[None], (count, *shard.shape)), axis...  16.6 us
    all_to_all x2, starting transfers between devices, sent_to_all(): lax.all_to_all(jnp.broadcast_to(shard[None], (count, *shard.shape)), axis...  11 us
    all_to_all x1, starting transfers between devices, sum_at_owner(): lax.all_to_all(parts, axis, split_axis=0, concat_axis=0, tiled=True)  10.3 us
    all_to_all x1, waiting for transfers between devices, sum_at_owner(): lax.all_to_all(parts, axis, split_axis=0, concat_axis=0, tiled=True)  7.7 us
    broadcast_in_dim x2, local copies, waits for them, and re-layouts, sent_to_all(): jnp.broadcast_to(shard[None], (count, *shard.shape))  2.15 us
  transfers between devices with their start and end apart: 3, of which 3 were waited for; matrix products, arithmetic and copies ran while one was open for 3% of the time, Pallas kernels for 0%

commit v1 on v0

v1 whole, which is shorter than its diff:
```python
import functools

import jax
import jax.numpy as jnp
from jax import lax
from jax.experimental import pallas as pl
from jax.experimental.pallas import tpu as pltpu
from jax.sharding import PartitionSpec as P

MESH = pl.DeviceIdType.MESH
F32 = jnp.float32
BF16 = jnp.bfloat16
OWN = 16
LANES = 128
PIECE = 5 * OWN + 8


def parts_of(x):
    first = x.astype(BF16).astype(F32)
    rest = x - first
    second = rest.astype(BF16).astype(F32)
    return first, second, (rest - second).astype(BF16).astype(F32)


def point_sums(ens_v, sums):
    @pl.loop(0, 16)
    def _(j):
        x = ens_v[:, pl.ds(pl.multiple_of(j * 1024, 1024), 1024)].astype(F32)
        total = jnp.sum(x, axis=0, keepdims=True)
        square = jnp.sum(x * x, axis=0, keepdims=True)
        piece = sums.at[(j // 2) % 2, j // 4]
        for i in range(8):
            row = 8 * (j % 2) + i
            piece[pl.ds(row, 1), :] = total[:, i * LANES : (i + 1) * LANES]
            piece[pl.ds(OWN + row, 1), :] = square[:, i * LANES : (i + 1) * LANES]


def histograms(val_v, var_v, pnt_v, acc, acc_q, sums):
    rows = 4
    across = (((1,), (1,)), ((), ()))
    acc[...] = jnp.zeros_like(acc)
    acc_q[...] = jnp.zeros_like(acc_q)

    @pl.loop(0, 32 // rows)
    def _(step):
        left, right, square = [], [], []
        for i in range(rows):
            at = pl.ds(step * rows + i, 1)
            point, value, var = pnt_v[at, :], val_v[at, :], var_v[at, :]
            index = lax.broadcasted_iota(jnp.int32, (LANES, LANES), 0)
            in_slot = index == point // LANES
            in_lane = index == point % LANES
            v1, v2, _ = parts_of(value)
            e1, e2, _ = parts_of(var)
            zero = jnp.zeros((LANES, LANES), F32)
            left.append(
                jnp.concatenate(
                    [
                        jnp.where(in_slot, jnp.broadcast_to(w, (LANES, LANES)), zero).astype(BF16)
                        for w in (jnp.ones_like(v1), v1, v2, e1, e2)
                    ],
                    axis=0,
                )
            )
            right.append(jnp.where(in_lane, 1.0, zero).astype(BF16))
            none = jnp.zeros_like(v1)
            square.append(
                jnp.concatenate(
                    [*parts_of(value * value), *parts_of(var * var), none, none], axis=0
                ).astype(BF16)
            )
        left = jnp.concatenate(left, axis=1)
        right = jnp.concatenate(right, axis=1)
        square = jnp.concatenate(square, axis=1)
        acc[...] += lax.dot_general(left, right, across, preferred_element_type=F32)
        acc_q[...] += lax.dot_general(square, left[:LANES], across, preferred_element_type=F32)

    for g in range(8):
        at = slice(g * OWN, (g + 1) * OWN)
        part = [acc[k * LANES + g * OWN : k * LANES + (g + 1) * OWN, :] for k in range(5)]
        piece = sums.at[g % 2, g // 2]
        piece[2 * OWN : 3 * OWN, :] = part[0]
        piece[3 * OWN : 4 * OWN, :] = part[1] + part[2]
        piece[4 * OWN : 5 * OWN, :] = part[3] + part[4]
        piece[5 * OWN :, :] = acc_q[...]


def kernel(
    ens, val, var, pnt, own, mean_tab, var_tab,
    out, post,
    ens_v, val_v, var_v, pnt_v, own_v, mean_v, ivar_v, out_v,
    acc, acc_q, sums, from_core, to_chip, from_chip, means, my_lam, lams, scale, to_region, from_region,
    load_sem, store_sem, core_send, core_recv, chip_send, chip_recv,
    mean_send, mean_recv, lam_send, lam_recv, reg_send, reg_recv,
):
    region, member = lax.axis_index("region"), lax.axis_index("member")
    regions, members = 32, 8
    y, core = member // 2, member % 2

    barrier = pltpu.get_barrier_semaphore()
    for d in range(1, regions):
        pl.semaphore_signal(
            barrier, inc=1, device_id={"region": (region + d) % regions}, device_id_type=MESH
        )
    for d in range(1, members):
        pl.semaphore_signal(
            barrier, inc=1, device_id={"member": (member + d) % members}, device_id_type=MESH
        )

    loads = [
        pltpu.make_async_copy(a, b, load_sem.at[i])
        for i, (a, b) in enumerate(
            (
                (ens, ens_v),
                (pnt, pnt_v),
                (val, val_v),
                (var, var_v),
                (own, own_v),
                (mean_tab, mean_v),
                (var_tab, ivar_v),
            )
        )
    ]
    for load in loads:
        load.start()
    for load in loads:
        load.wait()

    point_sums(ens_v, sums)
    histograms(val_v, var_v, pnt_v, acc, acc_q, sums)

    sub = lax.broadcasted_iota(jnp.int32, (LANES, LANES), 0)
    lane = lax.broadcasted_iota(jnp.int32, (LANES, LANES), 1)
    eye = sub == lane
    ids = own_v[...]
    ids_col = jnp.sum(jnp.where(eye, ids.astype(F32), 0.0), axis=1, keepdims=True).astype(jnp.int32)
    in_row = (
        lax.broadcasted_iota(jnp.int32, (LANES, 32), 1) == ids_col // LANES
    ).astype(F32)

    def looked_up(table):
        picked = jnp.dot(
            in_row, table[...], precision=lax.Precision.HIGHEST, preferred_element_type=F32
        )
        col = jnp.sum(jnp.where(lane == ids_col % LANES, picked, 0.0), axis=1, keepdims=True)
        return jnp.sum(jnp.where(eye, col, 0.0), axis=0, keepdims=True)

    prior_mean, prior_var = looked_up(mean_v), looked_up(ivar_v)

    pl.semaphore_wait(barrier, regions - 1 + members - 1)

    other = member + 1 - 2 * core
    order = (2, 1, 3, 0)
    core_copies = {}
    for d in order:
        at = (y + d) % 4
        core_copies[d] = pltpu.make_async_remote_copy(
            src_ref=sums.at[1 - core, at],
            dst_ref=from_core.at[d],
            send_sem=core_send.at[d],
            recv_sem=core_recv.at[d],
            device_id={"member": other},
            device_id_type=MESH,
        )
        core_copies[d].start()
    chip_copies = {}
    for d in order:
        core_copies[d].wait_recv()
        to_chip[d] = sums[core, (y + d) % 4] + from_core[d]
        if d:
            chip_copies[d] = pltpu.make_async_remote_copy(
                src_ref=to_chip.at[d],
                dst_ref=from_chip.at[d - 1],
                send_sem=chip_send.at[d - 1],
                recv_sem=chip_recv.at[d - 1],
                device_id={"member": ((y + d) % 4) * 2 + core},
                device_id_type=MESH,
            )
            chip_copies[d].start()
    for d in (1, 3, 2):
        chip_copies[d].wait_recv()

    def summed(k, size=OWN):
        at = slice(k * OWN, k * OWN + size)
        return (to_chip[0, at, :] + from_chip[0, at, :]) + (
            from_chip[1, at, :] + from_chip[2, at, :]
        )

    mean = summed(0) / 80.0
    my_rows = pl.ds(pl.multiple_of(member * OWN, OWN), OWN)
    means[my_rows, :] = mean
    mean_copies = []
    for d in (4, 3, 5, 2, 6, 1, 7):
        mean_copies.append(
            pltpu.make_async_remote_copy(
                src_ref=means.at[my_rows],
                dst_ref=means.at[my_rows],
                send_sem=mean_send.at[d - 1],
                recv_sem=mean_recv.at[d - 1],
                device_id={"member": (member + d) % members},
                device_id_type=MESH,
            )
        )
        mean_copies[-1].start()

    spread = (summed(1) - 80.0 * mean * mean) / 79.0
    count, value, error, squares = summed(2), summed(3), summed(4), summed(5, 8)
    mine = (
        lax.broadcasted_iota(jnp.int32, (OWN, LANES), 1)
        == lax.broadcasted_iota(jnp.int32, (OWN, LANES), 0) + member * OWN
    )

    def per_slot(x):
        col = jnp.sum(x, axis=1, keepdims=True)
        return jnp.sum(jnp.where(mine, col, 0.0), axis=0, keepdims=True)

    innov_sum = jnp.sum(squares[0:3], axis=0, keepdims=True) + per_slot(
        mean * (count * mean - 2.0 * value)
    )
    error_error = jnp.sum(squares[3:6], axis=0, keepdims=True)
    count_spread = count * spread
    spread_sum = per_slot(count_spread)
    spread_spread = per_slot(count_spread * spread)
    spread_error = per_slot(spread * error)
    error_sum = per_slot(error)
    weight_var = (
        2.0 * prior_mean * prior_mean * (1.0 + spread_spread)
        + 4.0 * prior_mean * spread_error
        + 2.0 * error_error
    )
    lam = jnp.maximum(
        (prior_mean * weight_var + prior_var * spread_sum * (innov_sum - error_sum))
        / (weight_var + prior_var * spread_sum * spread_sum),
        1.0,
    )
    lane_row = lax.broadcasted_iota(jnp.int32, (1, LANES), 1)
    my_lam[...] = jnp.where(lane_row // OWN == member, lam, 0.0)
    lam_copies = []
    for d in (4, 3, 5, 2, 6, 1, 7):
        lam_copies.append(
            pltpu.make_async_remote_copy(
                src_ref=my_lam,
                dst_ref=lams.at[d - 1],
                send_sem=lam_send.at[d - 1],
                recv_sem=lam_recv.at[d - 1],
                device_id={"member": (member + d) % members},
                device_id_type=MESH,
            )
        )
        lam_copies[-1].start()
    for copy in lam_copies:
        copy.wait_recv()
    lam_row = my_lam[...]
    for d in range(members - 1):
        lam_row = lam_row + lams[d]
    lam_col = jnp.sum(jnp.where(eye, lam_row, 0.0), axis=1, keepdims=True)

    for g in range(4):
        block = (g * 8 + lane // OWN) * LANES + member * OWN + lane % OWN
        to_region[g] = jnp.sum(jnp.where(ids_col == block, lam_col, 0.0), axis=0, keepdims=True)
    reg_copies = []
    for d in range(1, regions):
        dest = (region + d) % regions
        reg_copies.append(
            pltpu.make_async_remote_copy(
                src_ref=to_region.at[dest // 8],
                dst_ref=from_region.at[d - 1],
                send_sem=reg_send.at[d - 1],
                recv_sem=reg_recv.at[d - 1],
                device_id={"region": dest},
                device_id_type=MESH,
            )
        )
        reg_copies[-1].start()

    for copy in mean_copies:
        copy.wait_recv()
    scale[...] = jnp.broadcast_to(jnp.sqrt(lam_col), (LANES, LANES))

    @pl.loop(0, 16)
    def _(j):
        for i in range(8):
            at = pl.ds(pl.multiple_of(j * 1024 + i * LANES, LANES), LANES)
            row = pl.ds(j * 8 + i, 1)
            m = means[row, :]
            x = ens_v[:, at].astype(F32)
            out_v[:, at] = (m + scale[row, :] * (x - m)).astype(BF16)

    store = pltpu.make_async_copy(out_v, out, store_sem)
    store.start()

    for copy in reg_copies:
        copy.wait_recv()
    post_row = to_region[region // 8]
    for d in range(regions - 1):
        post_row = post_row + from_region[d]
    turned = pltpu.roll(
        jnp.broadcast_to(post_row, (8, LANES)), (8 - region % 8) * OWN % LANES, 1
    )
    post[...] = turned[0:1, :OWN]

    store.wait()
    for copy in (
        *core_copies.values(), *chip_copies.values(), *mean_copies, *lam_copies, *reg_copies
    ):
        copy.wait_send()


def body(ensemble, obs_value, obs_var, obs_point, owned_blocks, infl_mean, infl_var):
    anywhere = pl.BlockSpec(memory_space=pl.ANY)
    vmem = pl.BlockSpec(memory_space=pltpu.VMEM)
    dma = pltpu.SemaphoreType.DMA
    inflated, post = pl.pallas_call(
        kernel,
        out_shape=(
            jax.ShapeDtypeStruct(ensemble.shape, BF16),
            jax.ShapeDtypeStruct((1, OWN), F32),
        ),
        in_specs=[anywhere] * 7,
        out_specs=(anywhere, vmem),
        scratch_shapes=[
            pltpu.VMEM((10, 16384), BF16),
            pltpu.VMEM((32, LANES), F32),
            pltpu.VMEM((32, LANES), F32),
            pltpu.VMEM((32, LANES), jnp.int32),
            pltpu.VMEM((1, LANES), jnp.int32),
            pltpu.VMEM((32, LANES), F32),
            pltpu.VMEM((32, LANES), F32),
            pltpu.VMEM((10, 16384), BF16),
            pltpu.VMEM((5 * LANES, LANES), F32),
            pltpu.VMEM((8, LANES), F32),
            pltpu.VMEM((2, 4, PIECE, LANES), F32),
            pltpu.VMEM((4, PIECE, LANES), F32),
            pltpu.VMEM((4, PIECE, LANES), F32),
            pltpu.VMEM((3, PIECE, LANES), F32),
            pltpu.VMEM((LANES, LANES), F32),
            pltpu.VMEM((1, LANES), F32),
            pltpu.VMEM((7, 1, LANES), F32),
            pltpu.VMEM((LANES, LANES), F32),
            pltpu.VMEM((4, 1, LANES), F32),
            pltpu.VMEM((31, 1, LANES), F32),
            dma((7,)),
            dma,
            dma((4,)),
            dma((4,)),
            dma((3,)),
            dma((3,)),
            dma((7,)),
            dma((7,)),
            dma((7,)),
            dma((7,)),
            dma((31,)),
            dma((31,)),
        ],
        compiler_params=pltpu.CompilerParams(collective_id=0, has_side_effects=True),
    )(
        ensemble,
        obs_value,
        obs_var,
        obs_point,
        owned_blocks.reshape(1, -1),
        infl_mean.reshape(32, LANES),
        infl_var.reshape(32, LANES),
    )
    return inflated, post.reshape(-1)


def solution(mesh):
    placed = (
        P("member", "region"),
        P(("region", "member"), None),
        P(("region", "member"), None),
        P(("region", "member"), None),
        P("region"),
        P(),
        P(),
    )
    return jax.shard_map(
        body,
        mesh=mesh,
        in_specs=placed,
        out_specs=(P("member", "region"), P(("region", "member"))),
        check_vma=False,
    )
```

time: 105 us -> 32.5 us (0.31)
  local copies, waits for them, and re-layouts: 53.6 us -> 2.38 us
  Pallas kernels: 0 us -> 29.3 us
  waiting for transfers between devices: 24.3 us -> 0 us
  starting transfers between devices: 21.3 us -> 0 us
  other arithmetic: 3.4 us -> 0 us
  matrix products: 1.15 us -> 0 us
    gather x4 -> x0, local copies, waits for them, and re-layouts: 48.4 us -> none  [the longest x1 23 us: body(): at_mean = point_mean[own_points]]
    pallas_call x0 -> x1, Pallas kernels: none -> 29.3 us  [body(): pl.pallas_call(kernel, out_shape=(jax.ShapeDtypeStruct(ensemble.shape, BF...]
    all_to_all x3 -> x0, waiting for transfers between devices: 24.3 us -> none  [the longest x2 16.6 us: sent_to_all(): lax.all_to_all(jnp.broadcast_to(shard[None], (count, *shard.shape)), axis...]
    all_to_all x3 -> x0, starting transfers between devices: 21.3 us -> none  [the longest x2 11 us: sent_to_all(): lax.all_to_all(jnp.broadcast_to(shard[None], (count, *shard.shape)), axis...]
    reduce_sum x4 -> x0, other arithmetic: 2.25 us -> none  [the longest x1 1.46 us: body(): local_total = jnp.sum(wide, 0)]
    broadcast_in_dim x2 -> x0, local copies, waits for them, and re-layouts: 2.15 us -> none  [sent_to_all(): jnp.broadcast_to(shard[None], (count, *shard.shape))]
    unnamed x14 -> x4, local copies, waits for them, and re-layouts: 0.69 us -> 2.38 us
    scatter x1 -> x0, local copies, waits for them, and re-layouts: 1.58 us -> none  [body(): jnp.zeros((num_blocks,), jnp.float32).at[owned_blocks].set(lambda_owned)]
  transfers between devices with their start and end apart: 3 -> 0, of which waited for: 3 -> 0; matrix products, arithmetic and copies ran while one was open for 3% -> 0% of each run, Pallas kernels for 0% -> 0%
where the time goes in v1:
time: 32.5 us; the launch traced here: 32.4 us
  Pallas kernels  29.3 us (90%)
  local copies, waits for them, and re-layouts  2.38 us (7%)
  between operations  0.65 us (2%)
    pallas_call x1, Pallas kernels, body(): pl.pallas_call(kernel, out_shape=(jax.ShapeDtypeStruct(ensemble.shape, BF...  29.3 us
    unnamed x4, local copies, waits for them, and re-layouts  2.38 us

profile of v1, /device:TPU:1, one launch (start us, length us, event | category | flops | bytes accessed | tf_op | source)
XLA Modules:
  0.0 32.4 jit_solution(11906979108879152941)
XLA Ops:
  0.6 29.3 %shard_map.86 = (bf16[10,16384]{1,0:T(8,128)(2,1)}, f32[1,16]{1,0:T(1,128)}) custom-call(bf16[10,16384]{1,0:T(8,128)(2,1)} %ens.1, f32[32,128]{1,0:T(8,128)} %val.1, f32[32,128]{1,0:T(8,128)} %var.1, s32[32,128]{1,0:T(8,128)} %pnt.1, s32[1,128]{1,0:T(1,128)} %bitcast.6, f32[32,128]{1,0:T(8,128)} %bitcast.4, f32[32,128]{1,0:T(8,128)} %bitcast.5), custom_call_target="tpu_custom_call" | custom-call | tf_op jit(solution)/shard_map/pallas_call | solution.py:313
  30.0 0.0 copy-start
  30.0 1.9 %copy.11 = bf16[10,16384]{1,0:T(8,128)(2,1)} copy(bf16[10,16384]{1,0:T(8,128)(2,1)} %get-tuple-element.8) | data formatting | bytes 655360
  31.9 0.0 copy-done
  31.9 0.5 %copy.12 = f32[16]{0:T(128)} copy(f32[16]{0:T(128)S(1)} %bitcast.7) | data formatting | bytes 128
Async XLA Ops:
  30.0 1.9 %copy-start = (f32[1,16]{1,0:T(1,128)S(1)}, f32[1,16]{1,0:T(1,128)}, u32[]{:S(2)}) copy-start(f32[1,16]{1,0:T(1,128)} %get-tuple-element.5) | copy-start | bytes 196

commit v2 on v1

v2 whole, which is shorter than its diff:
```python
import jax
import jax.numpy as jnp
from jax import lax
from jax.experimental import pallas as pl
from jax.experimental.pallas import tpu as pltpu
from jax.sharding import PartitionSpec as P

MESH = pl.DeviceIdType.MESH
F32 = jnp.float32
BF16 = jnp.bfloat16
I32 = jnp.int32
OWN = 16
LANES = 128
HALF = 64
PIECE = 5 * OWN + 8
STEP = 8


def parts_of(x, count):
    parts = []
    for _ in range(count):
        parts.append(x.astype(BF16))
        x = x - parts[-1].astype(F32)
    return [p.astype(F32) for p in parts]


def point_sums(ens_v, sums):
    @pl.loop(0, 16)
    def _(j):
        x = ens_v[:, pl.ds(pl.multiple_of(j * 1024, 1024), 1024)].astype(F32)
        total = jnp.sum(x, axis=0, keepdims=True)
        square = jnp.sum(x * x, axis=0, keepdims=True)
        for i in range(8):
            row = 4 * (j % 4) + i // 2
            piece = sums.at[i % 2, j // 4]
            piece[pl.ds(row, 1), :] = total[:, i * LANES : (i + 1) * LANES]
            piece[pl.ds(OWN + row, 1), :] = square[:, i * LANES : (i + 1) * LANES]


def tall(row, rows):
    same = jnp.broadcast_to(row, (16, LANES)).astype(BF16)
    return jnp.concatenate([same] * (rows // 16), axis=0)


def histograms(val_v, var_v, pnt_v, acc, acc_q, sums):
    across = (((1,), (1,)), ((), ()))
    index = lax.broadcasted_iota(I32, (256, LANES), 0).astype(F32).astype(BF16)
    none, one = jnp.zeros((256, LANES), BF16), jnp.ones((256, LANES), BF16)
    acc[...] = jnp.zeros_like(acc)
    acc_q[...] = jnp.zeros_like(acc_q)

    @pl.loop(0, 32 // STEP)
    def _(step):
        left, right, square = [], [], []
        for i in range(STEP):
            at = pl.ds(step * STEP + i, 1)
            point, value, var = pnt_v[at, :], val_v[at, :], var_v[at, :]
            in_high = index[:HALF] == tall((point >> 8).astype(F32), HALF)
            in_low = index == tall((point & 255).astype(F32), 256)
            weights = [jnp.ones_like(value), *parts_of(value, 2), *parts_of(var, 2)]
            left.append(
                jnp.concatenate(
                    [jnp.where(in_high, tall(w, HALF), none[:HALF]) for w in weights], axis=0
                )
            )
            right.append(jnp.where(in_low, one, none))
            odd = ((point >> 7) & 1).astype(F32)
            parts = [*parts_of(value * value, 3), *parts_of(var * var, 3), jnp.zeros_like(value)]
            parts.append(parts[-1])
            square.append(
                jnp.concatenate(
                    [p * (1.0 - odd) for p in parts] + [p * odd for p in parts], axis=0
                ).astype(BF16)
            )
        left = jnp.concatenate(left, axis=1)
        right = jnp.concatenate(right, axis=1)
        square = jnp.concatenate(square, axis=1)
        acc[...] += lax.dot_general(left, right, across, preferred_element_type=F32)
        acc_q[...] += lax.dot_general(square, left[:HALF], across, preferred_element_type=F32)

    squares = jnp.concatenate([acc_q[:8, :], acc_q[8:, :]], axis=1)
    for parity in range(2):
        lanes = slice(parity * LANES, (parity + 1) * LANES)
        for y in range(4):
            part = [
                acc[k * HALF + y * OWN : k * HALF + (y + 1) * OWN, lanes] for k in range(5)
            ]
            piece = sums.at[parity, y]
            piece[2 * OWN : 3 * OWN, :] = part[0]
            piece[3 * OWN : 4 * OWN, :] = part[1] + part[2]
            piece[4 * OWN : 5 * OWN, :] = part[3] + part[4]
            piece[5 * OWN :, :] = squares


def looked_up(tables, own_v, ids_col):
    sub = lax.broadcasted_iota(I32, (LANES, LANES), 0)
    lane = lax.broadcasted_iota(I32, (LANES, LANES), 1)
    in_row = (lax.broadcasted_iota(I32, (LANES, 32), 1) == (ids_col >> 7)).astype(F32)
    rows = []
    for table in tables:
        picked = jnp.dot(
            in_row, table[...], precision=lax.Precision.HIGHEST, preferred_element_type=F32
        )
        col = jnp.sum(jnp.where(lane == (ids_col & 127), picked, 0.0), axis=1, keepdims=True)
        rows.append(jnp.sum(jnp.where(sub == lane, col, 0.0), axis=0, keepdims=True))
    return rows


def kernel(
    ens, val, var, pnt, own, mean_tab, var_tab,
    out, post,
    ens_v, val_v, var_v, pnt_v, own_v, mean_v, ivar_v,
    acc, acc_q, sums, from_core, to_chip, from_chip, means, my_lam, lams, scale, to_region, from_region,
    load_sem, core_send, core_recv, chip_send, chip_recv,
    mean_send, mean_recv, lam_send, lam_recv, reg_send, reg_recv,
):
    loads = [
        pltpu.make_async_copy(a, b, load_sem.at[i])
        for i, (a, b) in enumerate(
            (
                (ens, ens_v),
                (pnt, pnt_v),
                (val, val_v),
                (var, var_v),
                (own, own_v),
                (mean_tab, mean_v),
                (var_tab, ivar_v),
            )
        )
    ]
    for load in loads:
        load.start()

    region, member = lax.axis_index("region"), lax.axis_index("member")
    y, core = member // 2, member % 2
    ys = [y, *((y + d) % 4 for d in range(1, 4))]
    others = [2 * ys[d] + c for d in (2, 1, 3) for c in (core, 1 - core)] + [2 * y + 1 - core]
    xs = [8 * ((region // 8 + d) % 4) for d in range(4)]
    zs = [(region % 8 + d) % 8 for d in range(8)]
    far = sorted(
        ((dx, dz) for dx in range(4) for dz in range(8) if dx or dz),
        key=lambda d: -min(d[0], 4 - d[0]) - min(d[1], 8 - d[1]),
    )
    peers = [(xs[dx] + zs[dz], 8 * dx + dz - 1) for dx, dz in far]

    barrier = pltpu.get_barrier_semaphore()
    for peer, _ in peers:
        pl.semaphore_signal(barrier, inc=1, device_id={"region": peer}, device_id_type=MESH)
    for peer in others:
        pl.semaphore_signal(barrier, inc=1, device_id={"member": peer}, device_id_type=MESH)

    for load in loads:
        load.wait()

    point_sums(ens_v, sums)
    histograms(val_v, var_v, pnt_v, acc, acc_q, sums)

    pl.semaphore_wait(barrier, len(peers) + len(others))

    order = (2, 1, 3, 0)
    core_copies = {}
    for d in order:
        core_copies[d] = pltpu.make_async_remote_copy(
            src_ref=sums.at[1 - core, ys[d]],
            dst_ref=from_core.at[d],
            send_sem=core_send.at[d],
            recv_sem=core_recv.at[d],
            device_id={"member": 2 * y + 1 - core},
            device_id_type=MESH,
        )
        core_copies[d].start()
    chip_copies = {}
    for d in order:
        core_copies[d].wait_recv()
        to_chip[d] = sums[core, ys[d]] + from_core[d]
        if d:
            chip_copies[d] = pltpu.make_async_remote_copy(
                src_ref=to_chip.at[d],
                dst_ref=from_chip.at[d - 1],
                send_sem=chip_send.at[d - 1],
                recv_sem=chip_recv.at[d - 1],
                device_id={"member": 2 * ys[d] + core},
                device_id_type=MESH,
            )
            chip_copies[d].start()

    sub = lax.broadcasted_iota(I32, (LANES, LANES), 0)
    lane = lax.broadcasted_iota(I32, (LANES, LANES), 1)
    slot = 2 * (sub & (HALF - 1)) + (sub >> 6)
    ids_col = jnp.sum(
        jnp.where(lane == slot, own_v[...].astype(F32), 0.0), axis=1, keepdims=True
    ).astype(I32)
    prior_mean, prior_var = looked_up((mean_v, ivar_v), own_v, ids_col)
    blocks = [
        (8 * g + (lane >> 4)) * LANES + member * OWN + (lane & (OWN - 1)) == ids_col
        for g in range(4)
    ]

    for d in (1, 3, 2):
        chip_copies[d].wait_recv()

    def summed(k, size=OWN):
        at = slice(k * OWN, k * OWN + size)
        return (to_chip[0, at, :] + from_chip[0, at, :]) + (
            from_chip[1, at, :] + from_chip[2, at, :]
        )

    mean = summed(0) / 80.0
    first = core * HALF + y * OWN
    my_rows = pl.ds(pl.multiple_of(first, OWN), OWN)
    means[my_rows, :] = mean
    mean_copies = []
    for i, peer in enumerate(others):
        mean_copies.append(
            pltpu.make_async_remote_copy(
                src_ref=means.at[my_rows],
                dst_ref=means.at[my_rows],
                send_sem=mean_send.at[i],
                recv_sem=mean_recv.at[i],
                device_id={"member": peer},
                device_id_type=MESH,
            )
        )
        mean_copies[-1].start()

    spread = (summed(1) - 80.0 * mean * mean) / 79.0
    count, value, error, squares = summed(2), summed(3), summed(4), summed(5, 8)
    mine = (
        lax.broadcasted_iota(I32, (OWN, LANES), 1)
        == lax.broadcasted_iota(I32, (OWN, LANES), 0) + first
    )

    def per_slot(x):
        col = jnp.sum(x, axis=1, keepdims=True)
        return jnp.sum(jnp.where(mine, col, 0.0), axis=0, keepdims=True)

    innov_sum = jnp.sum(squares[0:3], axis=0, keepdims=True) + per_slot(
        mean * (count * mean - 2.0 * value)
    )
    error_error = jnp.sum(squares[3:6], axis=0, keepdims=True)
    count_spread = count * spread
    spread_sum = per_slot(count_spread)
    spread_spread = per_slot(count_spread * spread)
    spread_error = per_slot(spread * error)
    error_sum = per_slot(error)
    weight_var = (
        2.0 * prior_mean * prior_mean * (1.0 + spread_spread)
        + 4.0 * prior_mean * spread_error
        + 2.0 * error_error
    )
    lam = jnp.maximum(
        (prior_mean * weight_var + prior_var * spread_sum * (innov_sum - error_sum))
        / (weight_var + prior_var * spread_sum * spread_sum),
        1.0,
    )
    lane_row = lax.broadcasted_iota(I32, (1, LANES), 1)
    my_lam[...] = jnp.where((lane_row >= first) & (lane_row < first + OWN), lam, 0.0)
    lam_copies = []
    for i, peer in enumerate(others):
        lam_copies.append(
            pltpu.make_async_remote_copy(
                src_ref=my_lam,
                dst_ref=lams.at[i],
                send_sem=lam_send.at[i],
                recv_sem=lam_recv.at[i],
                device_id={"member": peer},
                device_id_type=MESH,
            )
        )
        lam_copies[-1].start()
    for copy in lam_copies:
        copy.wait_recv()
    lam_row = my_lam[...]
    for i in range(len(others)):
        lam_row = lam_row + lams[i]
    lam_col = jnp.sum(jnp.where(sub == lane, lam_row, 0.0), axis=1, keepdims=True)

    for g in range(4):
        to_region[g] = jnp.sum(jnp.where(blocks[g], lam_col, 0.0), axis=0, keepdims=True)
    reg_copies = []
    for peer, i in peers:
        reg_copies.append(
            pltpu.make_async_remote_copy(
                src_ref=to_region.at[peer // 8],
                dst_ref=from_region.at[i],
                send_sem=reg_send.at[i],
                recv_sem=reg_recv.at[i],
                device_id={"region": peer},
                device_id_type=MESH,
            )
        )
        reg_copies[-1].start()

    scale[...] = jnp.broadcast_to(jnp.sqrt(lam_col), (LANES, LANES))
    for copy in mean_copies:
        copy.wait_recv()

    @pl.loop(0, 16)
    def _(j):
        for i in range(8):
            at = pl.ds(pl.multiple_of(j * 1024 + i * LANES, LANES), LANES)
            row = pl.ds(HALF * (i % 2) + 4 * j + i // 2, 1)
            m = means[row, :]
            x = ens_v[:, at].astype(F32)
            out[:, at] = (m + scale[row, :] * (x - m)).astype(BF16)

    for copy in reg_copies:
        copy.wait_recv()
    post_row = to_region[region // 8]
    for i in range(len(peers)):
        post_row = post_row + from_region[i]
    turned = pltpu.roll(
        jnp.broadcast_to(post_row, (8, LANES)), (8 - region % 8) * OWN % LANES, 1
    )
    post[...] = turned[0:1, :OWN]

    for copy in (
        *core_copies.values(), *chip_copies.values(), *mean_copies, *lam_copies, *reg_copies
    ):
        copy.wait_send()


def body(ensemble, obs_value, obs_var, obs_point, owned_blocks, infl_mean, infl_var):
    anywhere = pl.BlockSpec(memory_space=pl.ANY)
    vmem = pl.BlockSpec(memory_space=pltpu.VMEM)
    dma = pltpu.SemaphoreType.DMA
    inflated, post = pl.pallas_call(
        kernel,
        out_shape=(pltpu.VMEM(ensemble.shape, BF16), pltpu.VMEM((1, OWN), F32)),
        in_specs=[anywhere] * 7,
        out_specs=(vmem, vmem),
        scratch_shapes=[
            pltpu.VMEM((10, 16384), BF16),
            pltpu.VMEM((32, LANES), F32),
            pltpu.VMEM((32, LANES), F32),
            pltpu.VMEM((32, LANES), I32),
            pltpu.VMEM((1, LANES), I32),
            pltpu.VMEM((32, LANES), F32),
            pltpu.VMEM((32, LANES), F32),
            pltpu.VMEM((5 * HALF, 2 * LANES), F32),
            pltpu.VMEM((16, HALF), F32),
            pltpu.VMEM((2, 4, PIECE, LANES), F32),
            pltpu.VMEM((4, PIECE, LANES), F32),
            pltpu.VMEM((4, PIECE, LANES), F32),
            pltpu.VMEM((3, PIECE, LANES), F32),
            pltpu.VMEM((LANES, LANES), F32),
            pltpu.VMEM((1, LANES), F32),
            pltpu.VMEM((7, 1, LANES), F32),
            pltpu.VMEM((LANES, LANES), F32),
            pltpu.VMEM((4, 1, LANES), F32),
            pltpu.VMEM((31, 1, LANES), F32),
            dma((7,)),
            *[dma((n,)) for n in (4, 3, 7, 7, 31) for _ in range(2)],
        ],
        compiler_params=pltpu.CompilerParams(collective_id=0, has_side_effects=True),
    )(
        ensemble,
        obs_value,
        obs_var,
        obs_point,
        owned_blocks.reshape(1, -1),
        infl_mean.reshape(32, LANES),
        infl_var.reshape(32, LANES),
    )
    return inflated, post.reshape(-1)


def solution(mesh):
    placed = (
        P("member", "region"),
        P(("region", "member"), None),
        P(("region", "member"), None),
        P(("region", "member"), None),
        P("region"),
        P(),
        P(),
    )
    return jax.shard_map(
        body,
        mesh=mesh,
        in_specs=placed,
        out_specs=(P("member", "region"), P(("region", "member"))),
        check_vma=False,
    )
```

time: 32.5 us -> 28.4 us (0.87)
  Pallas kernels: 29.3 us -> 26.4 us
  local copies, waits for them, and re-layouts: 2.38 us -> 1.31 us
    pallas_call x1, Pallas kernels: 29.3 us -> 26.4 us  [body(): pl.pallas_call(kernel, out_shape=(pltpu.VMEM(ensemble.shape, BF16), pltpu...]
    unnamed x4 -> x2, local copies, waits for them, and re-layouts: 2.38 us -> 1.31 us
where the time goes in v2:
time: 28.4 us; the launch traced here: 28.3 us
  Pallas kernels  26.4 us (93%)
  local copies, waits for them, and re-layouts  1.31 us (5%)
  between operations  0.64 us (2%)
    pallas_call x1, Pallas kernels, body(): pl.pallas_call(kernel, out_shape=(pltpu.VMEM(ensemble.shape, BF16), pltpu...  26.4 us
    unnamed x2, local copies, waits for them, and re-layouts  1.31 us

profile of v2, /device:TPU:1, one launch (start us, length us, event | category | flops | bytes accessed | tf_op | source)
XLA Modules:
  0.0 28.3 jit_solution(14821595150576375259)
XLA Ops:
  0.6 26.4 %shard_map.86 = (bf16[10,16384]{1,0:T(8,128)(2,1)S(1)}, f32[1,16]{1,0:T(1,128)S(1)}) custom-call(bf16[10,16384]{1,0:T(8,128)(2,1)} %ens.1, f32[32,128]{1,0:T(8,128)} %val.1, f32[32,128]{1,0:T(8,128)} %var.1, s32[32,128]{1,0:T(8,128)} %pnt.1, s32[1,128]{1,0:T(1,128)} %bitcast.7, f32[32,128]{1,0:T(8,128)} %bitcast.5, f32[32,128]{1,0:T(8,128)} %bitcast.6), custom_call_target="tpu_custom_call" | custom-call | tf_op jit(solution)/shard_map/pallas_call | solution.py:327
  27.0 0.8 %copy.11 = bf16[10,16384]{1,0:T(8,128)(2,1)} copy(bf16[10,16384]{1,0:T(8,128)(2,1)S(1)} %get-tuple-element.6) | data formatting | bytes 655360
  27.8 0.5 %copy.12 = f32[16]{0:T(128)} copy(f32[16]{0:T(128)S(1)} %bitcast.4) | data formatting | bytes 128

commit v3 on v2

--- a/solution.py
+++ b/solution.py
@@ -13,7 +13,7 @@
 LANES = 128
 HALF = 64
 PIECE = 5 * OWN + 8
-STEP = 8
+STEP = 16
 
 
 def parts_of(x, count):
@@ -209,20 +209,6 @@
     first = core * HALF + y * OWN
     my_rows = pl.ds(pl.multiple_of(first, OWN), OWN)
     means[my_rows, :] = mean
-    mean_copies = []
-    for i, peer in enumerate(others):
-        mean_copies.append(
-            pltpu.make_async_remote_copy(
-                src_ref=means.at[my_rows],
-                dst_ref=means.at[my_rows],
-                send_sem=mean_send.at[i],
-                recv_sem=mean_recv.at[i],
-                device_id={"member": peer},
-                device_id_type=MESH,
-            )
-        )
-        mean_copies[-1].start()
-
     spread = (summed(1) - 80.0 * mean * mean) / 79.0
     count, value, error, squares = summed(2), summed(3), summed(4), summed(5, 8)
     mine = (
@@ -268,6 +254,20 @@
             )
         )
         lam_copies[-1].start()
+    mean_copies = []
+    for i, peer in enumerate(others):
+        mean_copies.append(
+            pltpu.make_async_remote_copy(
+                src_ref=means.at[my_rows],
+                dst_ref=means.at[my_rows],
+                send_sem=mean_send.at[i],
+                recv_sem=mean_recv.at[i],
+                device_id={"member": peer},
+                device_id_type=MESH,
+            )
+        )
+        mean_copies[-1].start()
+
     for copy in lam_copies:
         copy.wait_recv()
     lam_row = my_lam[...]
@@ -318,6 +318,17 @@
         *core_copies.values(), *chip_copies.values(), *mean_copies, *lam_copies, *reg_copies
     ):
         copy.wait_send()
+
+
+def written(a, b, a_out, b_out, sem):
+    copies = [
+        pltpu.make_async_copy(a, a_out, sem.at[0]),
+        pltpu.make_async_copy(b, b_out, sem.at[1]),
+    ]
+    for copy in copies:
+        copy.start()
+    for copy in copies:
+        copy.wait()
 
 
 def body(ensemble, obs_value, obs_var, obs_point, owned_blocks, infl_mean, infl_var):
@@ -362,6 +373,19 @@
         infl_mean.reshape(32, LANES),
         infl_var.reshape(32, LANES),
     )
+    inflated, post = pl.pallas_call(
+        written,
+        out_shape=(
+            jax.ShapeDtypeStruct(ensemble.shape, BF16),
+            jax.ShapeDtypeStruct((1, OWN), F32),
+        ),
+        in_specs=(vmem, vmem),
+        out_specs=(anywhere, anywhere),
+        scratch_shapes=[dma((2,))],
+    )(
+        pltpu.with_memory_space_constraint(inflated, pltpu.VMEM),
+        pltpu.with_memory_space_constraint(post, pltpu.VMEM),
+    )
     return inflated, post.reshape(-1)
 
 

time: 28.4 us -> 27.2 us (0.958)
  local copies, waits for them, and re-layouts: 1.31 us -> 0 us
    unnamed x2 -> x0, local copies, waits for them, and re-layouts: 1.31 us -> none
    pallas_call x0 -> x1, Pallas kernels: none -> 0.81 us  [body(): pl.pallas_call(written, out_shape=(jax.ShapeDtypeStruct(ensemble.shape, B...]
    pallas_call x1, Pallas kernels: 26.4 us -> 25.6 us  [body(): pl.pallas_call(kernel, out_shape=(pltpu.VMEM(ensemble.shape, BF16), pltpu...]
where the time goes in v3:
time: 27.2 us; the launch traced here: 27.1 us
  Pallas kernels  26.5 us (97%)
  between operations  0.64 us (2%)
    pallas_call x1, Pallas kernels, body(): pl.pallas_call(kernel, out_shape=(pltpu.VMEM(ensemble.shape, BF16), pltpu...  25.6 us
    pallas_call x1, Pallas kernels, body(): pl.pallas_call(written, out_shape=(jax.ShapeDtypeStruct(ensemble.shape, B...  0.81 us

profile of v3, /device:TPU:1, one launch (start us, length us, event | category | flops | bytes accessed | tf_op | source)
XLA Modules:
  0.0 27.1 jit_solution(8073447546501214023)
XLA Ops:
  0.6 25.6 %shard_map.86 = (bf16[10,16384]{1,0:T(8,128)(2,1)S(1)}, f32[1,16]{1,0:T(1,128)S(1)}) custom-call(bf16[10,16384]{1,0:T(8,128)(2,1)} %ens.1, f32[32,128]{1,0:T(8,128)} %val.1, f32[32,128]{1,0:T(8,128)} %var.1, s32[32,128]{1,0:T(8,128)} %pnt.1, s32[1,128]{1,0:T(1,128)} %bitcast.6, f32[32,128]{1,0:T(8,128)} %bitcast.4, f32[32,128]{1,0:T(8,128)} %bitcast.5), custom_call_target="tpu_custom_call" | custom-call | tf_op jit(solution)/shard_map/pallas_call | solution.py:338
  26.3 0.8 %shard_map.87 = (bf16[10,16384]{1,0:T(8,128)(2,1)}, f32[1,16]{1,0:T(1,128)}) custom-call(bf16[10,16384]{1,0:T(8,128)(2,1)S(1)} %get-tuple-element.6.a, f32[1,16]{1,0:T(1,128)S(1)} %get-tuple-element.7.b), custom_call_target="tpu_custom_call" | custom-call | tf_op jit(solution)/shard_map/pallas_call | solution.py:376

commit v4 on v3

--- a/solution.py
+++ b/solution.py
@@ -92,18 +92,19 @@
             piece[5 * OWN :, :] = squares
 
 
-def looked_up(tables, own_v, ids_col):
-    sub = lax.broadcasted_iota(I32, (LANES, LANES), 0)
-    lane = lax.broadcasted_iota(I32, (LANES, LANES), 1)
-    in_row = (lax.broadcasted_iota(I32, (LANES, 32), 1) == (ids_col >> 7)).astype(F32)
-    rows = []
+def looked_up(tables, ids_col):
+    slots = ids_col.shape[0]
+    lane = lax.broadcasted_iota(I32, (slots, LANES), 1)
+    in_row = (lax.broadcasted_iota(I32, (slots, 32), 1) == (ids_col >> 7)).astype(F32)
+    cols = []
     for table in tables:
         picked = jnp.dot(
             in_row, table[...], precision=lax.Precision.HIGHEST, preferred_element_type=F32
         )
-        col = jnp.sum(jnp.where(lane == (ids_col & 127), picked, 0.0), axis=1, keepdims=True)
-        rows.append(jnp.sum(jnp.where(sub == lane, col, 0.0), axis=0, keepdims=True))
-    return rows
+        cols.append(
+            jnp.sum(jnp.where(lane == (ids_col & 127), picked, 0.0), axis=1, keepdims=True)
+        )
+    return cols
 
 
 def kernel(
@@ -141,10 +142,19 @@
         ((dx, dz) for dx in range(4) for dz in range(8) if dx or dz),
         key=lambda d: -min(d[0], 4 - d[0]) - min(d[1], 8 - d[1]),
     )
-    peers = [(xs[dx] + zs[dz], 8 * dx + dz - 1) for dx, dz in far]
+    regions = [xs[dx] + zs[dz] for dx, dz in far]
+    members = [2 * ys[d] + c for d in range(4) for c in (core, 1 - core)]
+    apart = sorted(
+        (
+            (-sum(min(a, n - a) for a, n in zip(d[:3], (4, 8, 4))), d)
+            for d in ((dx, dz, dy, c) for dx in range(4) for dz in range(8) for dy in range(4) for c in range(2))
+            if any(d)
+        )
+    )
+    peers = [(xs[dx] + zs[dz], members[2 * dy + c]) for _, (dx, dz, dy, c) in apart]
 
     barrier = pltpu.get_barrier_semaphore()
-    for peer, _ in peers:
+    for peer in regions:
         pl.semaphore_signal(barrier, inc=1, device_id={"region": peer}, device_id_type=MESH)
     for peer in others:
         pl.semaphore_signal(barrier, inc=1, device_id={"member": peer}, device_id_type=MESH)
@@ -155,7 +165,7 @@
     point_sums(ens_v, sums)
     histograms(val_v, var_v, pnt_v, acc, acc_q, sums)
 
-    pl.semaphore_wait(barrier, len(peers) + len(others))
+    pl.semaphore_wait(barrier, len(regions) + len(others))
 
     order = (2, 1, 3, 0)
     core_copies = {}
@@ -184,17 +194,15 @@
             )
             chip_copies[d].start()
 
-    sub = lax.broadcasted_iota(I32, (LANES, LANES), 0)
-    lane = lax.broadcasted_iota(I32, (LANES, LANES), 1)
-    slot = 2 * (sub & (HALF - 1)) + (sub >> 6)
+    sub = lax.broadcasted_iota(I32, (OWN, LANES), 0)
+    lane = lax.broadcasted_iota(I32, (OWN, LANES), 1)
     ids_col = jnp.sum(
-        jnp.where(lane == slot, own_v[...].astype(F32), 0.0), axis=1, keepdims=True
+        jnp.where(lane == 2 * (OWN * y + sub) + core, own_v[...].astype(F32), 0.0),
+        axis=1,
+        keepdims=True,
     ).astype(I32)
-    prior_mean, prior_var = looked_up((mean_v, ivar_v), own_v, ids_col)
-    blocks = [
-        (8 * g + (lane >> 4)) * LANES + member * OWN + (lane & (OWN - 1)) == ids_col
-        for g in range(4)
-    ]
+    prior_mean, prior_var = looked_up((mean_v, ivar_v), ids_col)
+    in_block = lane == (ids_col & 127)
 
     for d in (1, 3, 2):
         chip_copies[d].wait_recv()
@@ -211,19 +219,16 @@
     means[my_rows, :] = mean
     spread = (summed(1) - 80.0 * mean * mean) / 79.0
     count, value, error, squares = summed(2), summed(3), summed(4), summed(5, 8)
-    mine = (
-        lax.broadcasted_iota(I32, (OWN, LANES), 1)
-        == lax.broadcasted_iota(I32, (OWN, LANES), 0) + first
-    )
+    mine = lane == sub + first
 
     def per_slot(x):
-        col = jnp.sum(x, axis=1, keepdims=True)
-        return jnp.sum(jnp.where(mine, col, 0.0), axis=0, keepdims=True)
-
-    innov_sum = jnp.sum(squares[0:3], axis=0, keepdims=True) + per_slot(
-        mean * (count * mean - 2.0 * value)
-    )
-    error_error = jnp.sum(squares[3:6], axis=0, keepdims=True)
+        return jnp.sum(x, axis=1, keepdims=True)
+
+    innov_sum = per_slot(
+        jnp.where(mine, jnp.sum(squares[0:3], axis=0, keepdims=True), 0.0)
+        + mean * (count * mean - 2.0 * value)
+    )
+    error_error = per_slot(jnp.where(mine, jnp.sum(squares[3:6], axis=0, keepdims=True), 0.0))
     count_spread = count * spread
     spread_sum = per_slot(count_spread)
     spread_spread = per_slot(count_spread * spread)
@@ -239,8 +244,26 @@
         / (weight_var + prior_var * spread_sum * spread_sum),
         1.0,
     )
-    lane_row = lax.broadcasted_iota(I32, (1, LANES), 1)
-    my_lam[...] = jnp.where((lane_row >= first) & (lane_row < first + OWN), lam, 0.0)
+    placed = jnp.where(in_block, lam, 0.0)
+    for r in range(32):
+        to_region[r] = jnp.sum(
+            jnp.where((ids_col >> 7) == r, placed, 0.0), axis=0, keepdims=True
+        )
+    my_lam[...] = jnp.sum(jnp.where(mine, lam, 0.0), axis=0, keepdims=True)
+
+    def to_all(some):
+        for i, (peer, dest) in some:
+            pltpu.make_async_remote_copy(
+                src_ref=to_region.at[peer],
+                dst_ref=from_region.at[i],
+                send_sem=reg_send,
+                recv_sem=reg_recv,
+                device_id={"region": peer, "member": dest},
+                device_id_type=MESH,
+            ).start()
+
+    everyone = list(enumerate(peers))
+    to_all(everyone[:96])
     lam_copies = []
     for i, peer in enumerate(others):
         lam_copies.append(
@@ -268,29 +291,16 @@
         )
         mean_copies[-1].start()
 
+    to_all(everyone[96:])
     for copy in lam_copies:
         copy.wait_recv()
     lam_row = my_lam[...]
     for i in range(len(others)):
         lam_row = lam_row + lams[i]
-    lam_col = jnp.sum(jnp.where(sub == lane, lam_row, 0.0), axis=1, keepdims=True)
-
-    for g in range(4):
-        to_region[g] = jnp.sum(jnp.where(blocks[g], lam_col, 0.0), axis=0, keepdims=True)
-    reg_copies = []
-    for peer, i in peers:
-        reg_copies.append(
-            pltpu.make_async_remote_copy(
-                src_ref=to_region.at[peer // 8],
-                dst_ref=from_region.at[i],
-                send_sem=reg_send.at[i],
-                recv_sem=reg_recv.at[i],
-                device_id={"region": peer},
-                device_id_type=MESH,
-            )
-        )
-        reg_copies[-1].start()
-
+    eye = lax.broadcasted_iota(I32, (LANES, LANES), 0) == lax.broadcasted_iota(
+        I32, (LANES, LANES), 1
+    )
+    lam_col = jnp.sum(jnp.where(eye, lam_row, 0.0), axis=1, keepdims=True)
     scale[...] = jnp.broadcast_to(jnp.sqrt(lam_col), (LANES, LANES))
     for copy in mean_copies:
         copy.wait_recv()
@@ -304,18 +314,21 @@
             x = ens_v[:, at].astype(F32)
             out[:, at] = (m + scale[row, :] * (x - m)).astype(BF16)
 
-    for copy in reg_copies:
-        copy.wait_recv()
-    post_row = to_region[region // 8]
-    for i in range(len(peers)):
-        post_row = post_row + from_region[i]
-    turned = pltpu.roll(
-        jnp.broadcast_to(post_row, (8, LANES)), (8 - region % 8) * OWN % LANES, 1
-    )
+    arrived = pltpu.make_async_remote_copy(
+        src_ref=from_region,
+        dst_ref=from_region,
+        send_sem=reg_send,
+        recv_sem=reg_recv,
+        device_id={"member": others[0]},
+        device_id_type=MESH,
+    )
+    arrived.wait_recv()
+    post_row = to_region[region] + jnp.sum(from_region[...], axis=0)
+    turned = pltpu.roll(jnp.broadcast_to(post_row, (8, LANES)), (8 - member) * OWN % LANES, 1)
     post[...] = turned[0:1, :OWN]
 
     for copy in (
-        *core_copies.values(), *chip_copies.values(), *mean_copies, *lam_copies, *reg_copies
+        *core_copies.values(), *chip_copies.values(), *mean_copies, *lam_copies, arrived
     ):
         copy.wait_send()
 
@@ -358,10 +371,12 @@
             pltpu.VMEM((1, LANES), F32),
             pltpu.VMEM((7, 1, LANES), F32),
             pltpu.VMEM((LANES, LANES), F32),
-            pltpu.VMEM((4, 1, LANES), F32),
-            pltpu.VMEM((31, 1, LANES), F32),
+            pltpu.VMEM((32, 1, LANES), F32),
+            pltpu.VMEM((255, 1, LANES), F32),
             dma((7,)),
-            *[dma((n,)) for n in (4, 3, 7, 7, 31) for _ in range(2)],
+            *[dma((n,)) for n in (4, 3, 7, 7) for _ in range(2)],
+            dma,
+            dma,
         ],
         compiler_params=pltpu.CompilerParams(collective_id=0, has_side_effects=True),
     )(

time: 27.2 us -> 25.9 us (0.952)
  Pallas kernels: 26.5 us -> 25.2 us
    pallas_call x1, Pallas kernels: 25.6 us -> 24.4 us  [body(): pl.pallas_call(kernel, out_shape=(pltpu.VMEM(ensemble.shape, BF16), pltpu...]
where the time goes in v4:
time: 25.9 us; the launch traced here: 25.8 us
  Pallas kernels  25.2 us (97%)
  between operations  0.64 us (2%)
    pallas_call x1, Pallas kernels, body(): pl.pallas_call(kernel, out_shape=(pltpu.VMEM(ensemble.shape, BF16), pltpu...  24.4 us
    pallas_call x1, Pallas kernels, body(): pl.pallas_call(written, out_shape=(jax.ShapeDtypeStruct(ensemble.shape, B...  0.81 us

profile of v4, /device:TPU:1, one launch (start us, length us, event | category | flops | bytes accessed | tf_op | source)
XLA Modules:
  0.0 25.8 jit_solution(13763872128522106625)
XLA Ops:
  0.6 24.4 %shard_map.86 = (bf16[10,16384]{1,0:T(8,128)(2,1)S(1)}, f32[1,16]{1,0:T(1,128)S(1)}) custom-call(bf16[10,16384]{1,0:T(8,128)(2,1)} %ens.1, f32[32,128]{1,0:T(8,128)} %val.1, f32[32,128]{1,0:T(8,128)} %var.1, s32[32,128]{1,0:T(8,128)} %pnt.1, s32[1,128]{1,0:T(1,128)} %bitcast.6, f32[32,128]{1,0:T(8,128)} %bitcast.4, f32[32,128]{1,0:T(8,128)} %bitcast.5), custom_call_target="tpu_custom_call" | custom-call | tf_op jit(solution)/shard_map/pallas_call | solution.py:351
  25.0 0.8 %shard_map.87 = (bf16[10,16384]{1,0:T(8,128)(2,1)}, f32[1,16]{1,0:T(1,128)}) custom-call(bf16[10,16384]{1,0:T(8,128)(2,1)S(1)} %get-tuple-element.6.a, f32[1,16]{1,0:T(1,128)S(1)} %get-tuple-element.7.b), custom_call_target="tpu_custom_call" | custom-call | tf_op jit(solution)/shard_map/pallas_call | solution.py:391

commit v5 on v4

--- a/solution.py
+++ b/solution.py
@@ -12,7 +12,8 @@
 OWN = 16
 LANES = 128
 HALF = 64
-PIECE = 5 * OWN + 8
+POINTS = 2 * OWN
+COUNTS = 3 * OWN + 8
 STEP = 16
 
 
@@ -42,7 +43,7 @@
     return jnp.concatenate([same] * (rows // 16), axis=0)
 
 
-def histograms(val_v, var_v, pnt_v, acc, acc_q, sums):
+def histograms(val_v, var_v, pnt_v, acc, acc_q, counts):
     across = (((1,), (1,)), ((), ()))
     index = lax.broadcasted_iota(I32, (256, LANES), 0).astype(F32).astype(BF16)
     none, one = jnp.zeros((256, LANES), BF16), jnp.ones((256, LANES), BF16)
@@ -85,11 +86,11 @@
             part = [
                 acc[k * HALF + y * OWN : k * HALF + (y + 1) * OWN, lanes] for k in range(5)
             ]
-            piece = sums.at[parity, y]
-            piece[2 * OWN : 3 * OWN, :] = part[0]
-            piece[3 * OWN : 4 * OWN, :] = part[1] + part[2]
-            piece[4 * OWN : 5 * OWN, :] = part[3] + part[4]
-            piece[5 * OWN :, :] = squares
+            piece = counts.at[parity, y]
+            piece[:OWN, :] = part[0]
+            piece[OWN : 2 * OWN, :] = part[1] + part[2]
+            piece[2 * OWN : 3 * OWN, :] = part[3] + part[4]
+            piece[3 * OWN :, :] = squares
 
 
 def looked_up(tables, ids_col):
@@ -111,18 +112,18 @@
     ens, val, var, pnt, own, mean_tab, var_tab,
     out, post,
     ens_v, val_v, var_v, pnt_v, own_v, mean_v, ivar_v,
-    acc, acc_q, sums, from_core, to_chip, from_chip, means, my_lam, lams, scale, to_region, from_region,
-    load_sem, core_send, core_recv, chip_send, chip_recv,
+    acc, acc_q, sums, counts, sums_core, counts_core, sums_to, counts_to, sums_chip, counts_chip, means, my_lam, lams, scale, to_region, from_region,
+    load_sem, line_sem, all_sem, core_send, core_recv, chip_send, chip_recv,
     mean_send, mean_recv, lam_send, lam_recv, reg_send, reg_recv,
 ):
     loads = [
         pltpu.make_async_copy(a, b, load_sem.at[i])
         for i, (a, b) in enumerate(
             (
-                (ens, ens_v),
                 (pnt, pnt_v),
                 (val, val_v),
                 (var, var_v),
+                (ens, ens_v),
                 (own, own_v),
                 (mean_tab, mean_v),
                 (var_tab, ivar_v),
@@ -131,6 +132,7 @@
     ]
     for load in loads:
         load.start()
+    from_region[255:256, :] = jnp.zeros((1, LANES), F32)
 
     region, member = lax.axis_index("region"), lax.axis_index("member")
     y, core = member // 2, member % 2
@@ -138,11 +140,8 @@
     others = [2 * ys[d] + c for d in (2, 1, 3) for c in (core, 1 - core)] + [2 * y + 1 - core]
     xs = [8 * ((region // 8 + d) % 4) for d in range(4)]
     zs = [(region % 8 + d) % 8 for d in range(8)]
-    far = sorted(
-        ((dx, dz) for dx in range(4) for dz in range(8) if dx or dz),
-        key=lambda d: -min(d[0], 4 - d[0]) - min(d[1], 8 - d[1]),
-    )
-    regions = [xs[dx] + zs[dz] for dx, dz in far]
+    along_x = [xs[d] + zs[0] for d in (2, 1, 3)]
+    along_z = [xs[0] + zs[d] for d in (4, 3, 5, 2, 6, 1, 7)]
     members = [2 * ys[d] + c for d in range(4) for c in (core, 1 - core)]
     apart = sorted(
         (
@@ -154,45 +153,60 @@
     peers = [(xs[dx] + zs[dz], members[2 * dy + c]) for _, (dx, dz, dy, c) in apart]
 
     barrier = pltpu.get_barrier_semaphore()
-    for peer in regions:
-        pl.semaphore_signal(barrier, inc=1, device_id={"region": peer}, device_id_type=MESH)
     for peer in others:
         pl.semaphore_signal(barrier, inc=1, device_id={"member": peer}, device_id_type=MESH)
-
-    for load in loads:
+    for peer in (*along_x, *along_z[3:]):
+        pl.semaphore_signal(barrier, inc=1, device_id={"region": peer}, device_id_type=MESH)
+
+    for load in loads[:3]:
         load.wait()
-
-    point_sums(ens_v, sums)
-    histograms(val_v, var_v, pnt_v, acc, acc_q, sums)
-
-    pl.semaphore_wait(barrier, len(regions) + len(others))
+    histograms(val_v, var_v, pnt_v, acc, acc_q, counts)
+
+    pl.semaphore_wait(barrier, len(others) + len(along_x) + 4)
 
     order = (2, 1, 3, 0)
-    core_copies = {}
-    for d in order:
-        core_copies[d] = pltpu.make_async_remote_copy(
-            src_ref=sums.at[1 - core, ys[d]],
-            dst_ref=from_core.at[d],
-            send_sem=core_send.at[d],
-            recv_sem=core_recv.at[d],
+    def core_copy(k, d):
+        return pltpu.make_async_remote_copy(
+            src_ref=(sums, counts)[k].at[1 - core, ys[d]],
+            dst_ref=(sums_core, counts_core)[k].at[d],
+            send_sem=core_send.at[4 * k + d],
+            recv_sem=core_recv.at[4 * k + d],
             device_id={"member": 2 * y + 1 - core},
             device_id_type=MESH,
         )
-        core_copies[d].start()
-    chip_copies = {}
+
+    def chip_copy(k, d):
+        return pltpu.make_async_remote_copy(
+            src_ref=(sums_to, counts_to)[k].at[d],
+            dst_ref=(sums_chip, counts_chip)[k].at[d - 1],
+            send_sem=chip_send.at[3 * k + d - 1],
+            recv_sem=chip_recv.at[3 * k + d - 1],
+            device_id={"member": 2 * ys[d] + core},
+            device_id_type=MESH,
+        )
+
+    def pass_on(k):
+        own, came, total = ((sums, sums_core, sums_to), (counts, counts_core, counts_to))[k]
+        for d in order:
+            core_copy(k, d).wait_recv()
+            total[d] = own[core, ys[d]] + came[d]
+            if d:
+                chip_copy(k, d).start()
+
     for d in order:
-        core_copies[d].wait_recv()
-        to_chip[d] = sums[core, ys[d]] + from_core[d]
-        if d:
-            chip_copies[d] = pltpu.make_async_remote_copy(
-                src_ref=to_chip.at[d],
-                dst_ref=from_chip.at[d - 1],
-                send_sem=chip_send.at[d - 1],
-                recv_sem=chip_recv.at[d - 1],
-                device_id={"member": 2 * ys[d] + core},
-                device_id_type=MESH,
-            )
-            chip_copies[d].start()
+        core_copy(1, d).start()
+    for peer in (*along_x, *along_z[3:5]):
+        pl.semaphore_signal(line_sem, inc=1, device_id={"region": peer}, device_id_type=MESH)
+    for load in loads[3:]:
+        load.wait()
+    point_sums(ens_v, sums)
+    for d in order:
+        core_copy(0, d).start()
+    pass_on(1)
+    pass_on(0)
+    pl.semaphore_wait(line_sem, len(along_x) + 2)
+    for peer in along_z:
+        pl.semaphore_signal(all_sem, inc=1, device_id={"region": peer}, device_id_type=MESH)
 
     sub = lax.broadcasted_iota(I32, (OWN, LANES), 0)
     lane = lax.broadcasted_iota(I32, (OWN, LANES), 1)
@@ -204,21 +218,21 @@
     prior_mean, prior_var = looked_up((mean_v, ivar_v), ids_col)
     in_block = lane == (ids_col & 127)
 
-    for d in (1, 3, 2):
-        chip_copies[d].wait_recv()
-
-    def summed(k, size=OWN):
+    for k in (1, 0):
+        for d in (1, 3, 2):
+            chip_copy(k, d).wait_recv()
+
+    def summed(total, came, k, size=OWN):
         at = slice(k * OWN, k * OWN + size)
-        return (to_chip[0, at, :] + from_chip[0, at, :]) + (
-            from_chip[1, at, :] + from_chip[2, at, :]
-        )
-
-    mean = summed(0) / 80.0
+        return (total[0, at, :] + came[0, at, :]) + (came[1, at, :] + came[2, at, :])
+
+    mean = summed(sums_to, sums_chip, 0) / 80.0
     first = core * HALF + y * OWN
     my_rows = pl.ds(pl.multiple_of(first, OWN), OWN)
     means[my_rows, :] = mean
-    spread = (summed(1) - 80.0 * mean * mean) / 79.0
-    count, value, error, squares = summed(2), summed(3), summed(4), summed(5, 8)
+    spread = (summed(sums_to, sums_chip, 1) - 80.0 * mean * mean) / 79.0
+    count, value, error = (summed(counts_to, counts_chip, k) for k in range(3))
+    squares = summed(counts_to, counts_chip, 3, 8)
     mine = lane == sub + first
 
     def per_slot(x):
@@ -255,7 +269,7 @@
         for i, (peer, dest) in some:
             pltpu.make_async_remote_copy(
                 src_ref=to_region.at[peer],
-                dst_ref=from_region.at[i],
+                dst_ref=from_region.at[pl.ds(i, 1)],
                 send_sem=reg_send,
                 recv_sem=reg_recv,
                 device_id={"region": peer, "member": dest},
@@ -263,6 +277,7 @@
             ).start()
 
     everyone = list(enumerate(peers))
+    pl.semaphore_wait(all_sem, len(along_z))
     to_all(everyone[:96])
     lam_copies = []
     for i, peer in enumerate(others):
@@ -315,21 +330,24 @@
             out[:, at] = (m + scale[row, :] * (x - m)).astype(BF16)
 
     arrived = pltpu.make_async_remote_copy(
-        src_ref=from_region,
-        dst_ref=from_region,
+        src_ref=from_region.at[0:255],
+        dst_ref=from_region.at[0:255],
         send_sem=reg_send,
         recv_sem=reg_recv,
         device_id={"member": others[0]},
         device_id_type=MESH,
     )
     arrived.wait_recv()
-    post_row = to_region[region] + jnp.sum(from_region[...], axis=0)
+    post_row = to_region[region] + jnp.sum(from_region[...], axis=0, keepdims=True)
     turned = pltpu.roll(jnp.broadcast_to(post_row, (8, LANES)), (8 - member) * OWN % LANES, 1)
     post[...] = turned[0:1, :OWN]
 
-    for copy in (
-        *core_copies.values(), *chip_copies.values(), *mean_copies, *lam_copies, arrived
-    ):
+    for k in range(2):
+        for d in order:
+            core_copy(k, d).wait_send()
+            if d:
+                chip_copy(k, d).wait_send()
+    for copy in (*mean_copies, *lam_copies, arrived):
         copy.wait_send()
 
 
@@ -363,18 +381,21 @@
             pltpu.VMEM((32, LANES), F32),
             pltpu.VMEM((5 * HALF, 2 * LANES), F32),
             pltpu.VMEM((16, HALF), F32),
-            pltpu.VMEM((2, 4, PIECE, LANES), F32),
-            pltpu.VMEM((4, PIECE, LANES), F32),
-            pltpu.VMEM((4, PIECE, LANES), F32),
-            pltpu.VMEM((3, PIECE, LANES), F32),
+            *[
+                pltpu.VMEM((*lead, rows, LANES), F32)
+                for lead in ((2, 4), (4,), (4,), (3,))
+                for rows in (POINTS, COUNTS)
+            ],
             pltpu.VMEM((LANES, LANES), F32),
             pltpu.VMEM((1, LANES), F32),
             pltpu.VMEM((7, 1, LANES), F32),
             pltpu.VMEM((LANES, LANES), F32),
             pltpu.VMEM((32, 1, LANES), F32),
-            pltpu.VMEM((255, 1, LANES), F32),
+            pltpu.VMEM((256, LANES), F32),
             dma((7,)),
-            *[dma((n,)) for n in (4, 3, 7, 7) for _ in range(2)],
+            pltpu.SemaphoreType.REGULAR,
+            pltpu.SemaphoreType.REGULAR,
+            *[dma((n,)) for n in (8, 6, 7, 7) for _ in range(2)],
             dma,
             dma,
         ],

time: 25.9 us -> 25.4 us (0.981)
  Pallas kernels: 25.2 us -> 24.5 us
    pallas_call x1, Pallas kernels: 24.4 us -> 23.7 us  [body(): pl.pallas_call(kernel, out_shape=(pltpu.VMEM(ensemble.shape, BF16), pltpu...]
where the time goes in v5:
time: 25.4 us; the launch traced here: 25.2 us
  Pallas kernels  24.5 us (96%)
  between operations  0.64 us (3%)
    pallas_call x1, Pallas kernels, body(): pl.pallas_call(kernel, out_shape=(pltpu.VMEM(ensemble.shape, BF16), pltpu...  23.7 us
    pallas_call x1, Pallas kernels, body(): pl.pallas_call(written, out_shape=(jax.ShapeDtypeStruct(ensemble.shape, B...  0.81 us

profile of v5, /device:TPU:1, one launch (start us, length us, event | category | flops | bytes accessed | tf_op | source)
XLA Modules:
  0.0 25.2 jit_solution(18366027338008537785)
XLA Ops:
  0.6 23.7 %shard_map.86 = (bf16[10,16384]{1,0:T(8,128)(2,1)S(1)}, f32[1,16]{1,0:T(1,128)S(1)}) custom-call(bf16[10,16384]{1,0:T(8,128)(2,1)} %ens.1, f32[32,128]{1,0:T(8,128)} %val.1, f32[32,128]{1,0:T(8,128)} %var.1, s32[32,128]{1,0:T(8,128)} %pnt.1, s32[1,128]{1,0:T(1,128)} %bitcast.6, f32[32,128]{1,0:T(8,128)} %bitcast.4, f32[32,128]{1,0:T(8,128)} %bitcast.5), custom_call_target="tpu_custom_call" | custom-call | tf_op jit(solution)/shard_map/pallas_call | solution.py:369
  24.4 0.8 %shard_map.87 = (bf16[10,16384]{1,0:T(8,128)(2,1)}, f32[1,16]{1,0:T(1,128)}) custom-call(bf16[10,16384]{1,0:T(8,128)(2,1)S(1)} %get-tuple-element.6.a, f32[1,16]{1,0:T(1,128)S(1)} %get-tuple-element.7.b), custom_call_target="tpu_custom_call" | custom-call | tf_op jit(solution)/shard_map/pallas_call | solution.py:412

commit v6 on v5

--- a/solution.py
+++ b/solution.py
@@ -14,7 +14,7 @@
 HALF = 64
 POINTS = 2 * OWN
 COUNTS = 3 * OWN + 8
-STEP = 16
+STEP = 32
 
 
 def parts_of(x, count):
@@ -43,43 +43,66 @@
     return jnp.concatenate([same] * (rows // 16), axis=0)
 
 
-def histograms(val_v, var_v, pnt_v, acc, acc_q, counts):
+def histograms(val_v, var_v, pnt_v, rows_v, acc, acc_q, counts):
     across = (((1,), (1,)), ((), ()))
+    point, value, var = pnt_v[...], val_v[...], var_v[...]
+    odd = ((point >> 7) & 1).astype(F32)
+    squares = [*parts_of(value * value, 2), *parts_of(var * var, 2)]
+    kinds = [
+        (point >> 8).astype(F32),
+        (point & 255).astype(F32),
+        *parts_of(value, 2),
+        *parts_of(var, 2),
+        *(p * (1.0 - odd) for p in squares),
+        *(p * odd for p in squares),
+    ]
+    for k, kind in enumerate(kinds):
+        rows_v[k] = kind
     index = lax.broadcasted_iota(I32, (256, LANES), 0).astype(F32).astype(BF16)
     none, one = jnp.zeros((256, LANES), BF16), jnp.ones((256, LANES), BF16)
-    acc[...] = jnp.zeros_like(acc)
-    acc_q[...] = jnp.zeros_like(acc_q)
-
-    @pl.loop(0, 32 // STEP)
-    def _(step):
+    sub = lax.broadcasted_iota(I32, (8, LANES), 0)
+
+    def step(first):
         left, right, square = [], [], []
         for i in range(STEP):
-            at = pl.ds(step * STEP + i, 1)
-            point, value, var = pnt_v[at, :], val_v[at, :], var_v[at, :]
-            in_high = index[:HALF] == tall((point >> 8).astype(F32), HALF)
-            in_low = index == tall((point & 255).astype(F32), 256)
-            weights = [jnp.ones_like(value), *parts_of(value, 2), *parts_of(var, 2)]
+            row = [rows_v[k, pl.ds(first + i, 1), :] for k in range(14)]
+            in_high = index[:HALF] == tall(row[0], HALF)
+            in_low = index == tall(row[1], 256)
             left.append(
                 jnp.concatenate(
-                    [jnp.where(in_high, tall(w, HALF), none[:HALF]) for w in weights], axis=0
+                    [
+                        jnp.where(in_high, one[:HALF], none[:HALF]),
+                        *(jnp.where(in_high, tall(w, HALF), none[:HALF]) for w in row[2:6]),
+                    ],
+                    axis=0,
                 )
             )
             right.append(jnp.where(in_low, one, none))
-            odd = ((point >> 7) & 1).astype(F32)
-            parts = [*parts_of(value * value, 3), *parts_of(var * var, 3), jnp.zeros_like(value)]
-            parts.append(parts[-1])
-            square.append(
-                jnp.concatenate(
-                    [p * (1.0 - odd) for p in parts] + [p * odd for p in parts], axis=0
-                ).astype(BF16)
-            )
+            stack = jnp.broadcast_to(row[6], (8, LANES))
+            for k in range(1, 8):
+                stack = jnp.where(sub == k, row[6 + k], stack)
+            square.append(stack)
         left = jnp.concatenate(left, axis=1)
         right = jnp.concatenate(right, axis=1)
-        square = jnp.concatenate(square, axis=1)
-        acc[...] += lax.dot_general(left, right, across, preferred_element_type=F32)
-        acc_q[...] += lax.dot_general(square, left[:HALF], across, preferred_element_type=F32)
-
-    squares = jnp.concatenate([acc_q[:8, :], acc_q[8:, :]], axis=1)
+        square = jnp.concatenate(square, axis=1).astype(BF16)
+        return (
+            lax.dot_general(left, right, across, preferred_element_type=F32),
+            lax.dot_general(square, left[:HALF], across, preferred_element_type=F32),
+        )
+
+    if STEP == 32:
+        acc[...], acc_q[...] = step(0)
+    else:
+        acc[...], acc_q[...] = jnp.zeros_like(acc), jnp.zeros_like(acc_q)
+
+        @pl.loop(0, 32 // STEP)
+        def _(i):
+            more, more_q = step(i * STEP)
+            acc[...] += more
+            acc_q[...] += more_q
+
+    squares = jnp.concatenate([acc_q[:4, :], acc_q[4:, :]], axis=1)
+    squares = jnp.concatenate([squares, squares], axis=0)
     for parity in range(2):
         lanes = slice(parity * LANES, (parity + 1) * LANES)
         for y in range(4):
@@ -112,7 +135,7 @@
     ens, val, var, pnt, own, mean_tab, var_tab,
     out, post,
     ens_v, val_v, var_v, pnt_v, own_v, mean_v, ivar_v,
-    acc, acc_q, sums, counts, sums_core, counts_core, sums_to, counts_to, sums_chip, counts_chip, means, my_lam, lams, scale, to_region, from_region,
+    rows_v, acc, acc_q, sums, counts, sums_core, counts_core, sums_to, counts_to, sums_chip, counts_chip, means, my_lam, lams, scale, to_region, from_region,
     load_sem, line_sem, all_sem, core_send, core_recv, chip_send, chip_recv,
     mean_send, mean_recv, lam_send, lam_recv, reg_send, reg_recv,
 ):
@@ -135,11 +158,12 @@
     from_region[255:256, :] = jnp.zeros((1, LANES), F32)
 
     region, member = lax.axis_index("region"), lax.axis_index("member")
-    y, core = member // 2, member % 2
-    ys = [y, *((y + d) % 4 for d in range(1, 4))]
+    y, core = lax.div(member, 2), lax.rem(member, 2)
+    ys = [y, *(lax.rem(y + d, 4) for d in range(1, 4))]
     others = [2 * ys[d] + c for d in (2, 1, 3) for c in (core, 1 - core)] + [2 * y + 1 - core]
-    xs = [8 * ((region // 8 + d) % 4) for d in range(4)]
-    zs = [(region % 8 + d) % 8 for d in range(8)]
+    x, z = lax.div(region, 8), lax.rem(region, 8)
+    xs = [8 * lax.rem(x + d, 4) for d in range(4)]
+    zs = [lax.rem(z + d, 8) for d in range(8)]
     along_x = [xs[d] + zs[0] for d in (2, 1, 3)]
     along_z = [xs[0] + zs[d] for d in (4, 3, 5, 2, 6, 1, 7)]
     members = [2 * ys[d] + c for d in range(4) for c in (core, 1 - core)]
@@ -153,18 +177,20 @@
     peers = [(xs[dx] + zs[dz], members[2 * dy + c]) for _, (dx, dz, dy, c) in apart]
 
     barrier = pltpu.get_barrier_semaphore()
+    for peer in (along_x[0], *along_z[3:5]):
+        pl.semaphore_signal(barrier, inc=1, device_id={"region": peer}, device_id_type=MESH)
     for peer in others:
         pl.semaphore_signal(barrier, inc=1, device_id={"member": peer}, device_id_type=MESH)
-    for peer in (*along_x, *along_z[3:]):
+    for peer in (*along_x[1:], *along_z[5:]):
         pl.semaphore_signal(barrier, inc=1, device_id={"region": peer}, device_id_type=MESH)
 
     for load in loads[:3]:
         load.wait()
-    histograms(val_v, var_v, pnt_v, acc, acc_q, counts)
+    histograms(val_v, var_v, pnt_v, rows_v, acc, acc_q, counts)
 
     pl.semaphore_wait(barrier, len(others) + len(along_x) + 4)
 
-    order = (2, 1, 3, 0)
+    order = (1, 3, 0)
     def core_copy(k, d):
         return pltpu.make_async_remote_copy(
             src_ref=(sums, counts)[k].at[1 - core, ys[d]],
@@ -175,15 +201,19 @@
             device_id_type=MESH,
         )
 
-    def chip_copy(k, d):
+    def chip_copy(k, d, turn=0):
+        i = 3 if turn else d - 1
+        to = 1 - core if turn else core
         return pltpu.make_async_remote_copy(
-            src_ref=(sums_to, counts_to)[k].at[d],
-            dst_ref=(sums_chip, counts_chip)[k].at[d - 1],
-            send_sem=chip_send.at[3 * k + d - 1],
-            recv_sem=chip_recv.at[3 * k + d - 1],
-            device_id={"member": 2 * ys[d] + core},
+            src_ref=(sums, counts)[k].at[to, ys[2]] if d == 2 else (sums_to, counts_to)[k].at[d],
+            dst_ref=(sums_chip, counts_chip)[k].at[i],
+            send_sem=chip_send.at[4 * k + i],
+            recv_sem=chip_recv.at[4 * k + i],
+            device_id={"member": 2 * ys[d] + to},
             device_id_type=MESH,
         )
+
+    chip_copies = [(k, d, turn) for k in (1, 0) for d, turn in ((1, 0), (3, 0), (2, 0), (2, 1))]
 
     def pass_on(k):
         own, came, total = ((sums, sums_core, sums_to), (counts, counts_core, counts_to))[k]
@@ -195,6 +225,8 @@
 
     for d in order:
         core_copy(1, d).start()
+    for turn in range(2):
+        chip_copy(1, 2, turn).start()
     for peer in (*along_x, *along_z[3:5]):
         pl.semaphore_signal(line_sem, inc=1, device_id={"region": peer}, device_id_type=MESH)
     for load in loads[3:]:
@@ -202,6 +234,8 @@
     point_sums(ens_v, sums)
     for d in order:
         core_copy(0, d).start()
+    for turn in range(2):
+        chip_copy(0, 2, turn).start()
     pass_on(1)
     pass_on(0)
     pl.semaphore_wait(line_sem, len(along_x) + 2)
@@ -218,13 +252,13 @@
     prior_mean, prior_var = looked_up((mean_v, ivar_v), ids_col)
     in_block = lane == (ids_col & 127)
 
-    for k in (1, 0):
-        for d in (1, 3, 2):
-            chip_copy(k, d).wait_recv()
+    for copy in chip_copies:
+        chip_copy(*copy).wait_recv()
 
     def summed(total, came, k, size=OWN):
         at = slice(k * OWN, k * OWN + size)
-        return (total[0, at, :] + came[0, at, :]) + (came[1, at, :] + came[2, at, :])
+        near = total[0, at, :] + (came[0, at, :] + came[2, at, :])
+        return near + (came[1, at, :] + came[3, at, :])
 
     mean = summed(sums_to, sums_chip, 0) / 80.0
     first = core * HALF + y * OWN
@@ -239,10 +273,10 @@
         return jnp.sum(x, axis=1, keepdims=True)
 
     innov_sum = per_slot(
-        jnp.where(mine, jnp.sum(squares[0:3], axis=0, keepdims=True), 0.0)
+        jnp.where(mine, jnp.sum(squares[0:2], axis=0, keepdims=True), 0.0)
         + mean * (count * mean - 2.0 * value)
     )
-    error_error = per_slot(jnp.where(mine, jnp.sum(squares[3:6], axis=0, keepdims=True), 0.0))
+    error_error = per_slot(jnp.where(mine, jnp.sum(squares[2:4], axis=0, keepdims=True), 0.0))
     count_spread = count * spread
     spread_sum = per_slot(count_spread)
     spread_spread = per_slot(count_spread * spread)
@@ -337,18 +371,17 @@
         device_id={"member": others[0]},
         device_id_type=MESH,
     )
+    for k in range(2):
+        for d in order:
+            core_copy(k, d).wait_send()
+    for copy in chip_copies:
+        chip_copy(*copy).wait_send()
+    for copy in (*mean_copies, *lam_copies, arrived):
+        copy.wait_send()
     arrived.wait_recv()
     post_row = to_region[region] + jnp.sum(from_region[...], axis=0, keepdims=True)
     turned = pltpu.roll(jnp.broadcast_to(post_row, (8, LANES)), (8 - member) * OWN % LANES, 1)
     post[...] = turned[0:1, :OWN]
-
-    for k in range(2):
-        for d in order:
-            core_copy(k, d).wait_send()
-            if d:
-                chip_copy(k, d).wait_send()
-    for copy in (*mean_copies, *lam_copies, arrived):
-        copy.wait_send()
 
 
 def written(a, b, a_out, b_out, sem):
@@ -379,11 +412,12 @@
             pltpu.VMEM((1, LANES), I32),
             pltpu.VMEM((32, LANES), F32),
             pltpu.VMEM((32, LANES), F32),
+            pltpu.VMEM((14, 32, LANES), F32),
             pltpu.VMEM((5 * HALF, 2 * LANES), F32),
-            pltpu.VMEM((16, HALF), F32),
+            pltpu.VMEM((8, HALF), F32),
             *[
                 pltpu.VMEM((*lead, rows, LANES), F32)
-                for lead in ((2, 4), (4,), (4,), (3,))
+                for lead in ((2, 4), (4,), (4,), (4,))
                 for rows in (POINTS, COUNTS)
             ],
             pltpu.VMEM((LANES, LANES), F32),
@@ -395,7 +429,7 @@
             dma((7,)),
             pltpu.SemaphoreType.REGULAR,
             pltpu.SemaphoreType.REGULAR,
-            *[dma((n,)) for n in (8, 6, 7, 7) for _ in range(2)],
+            *[dma((n,)) for n in (8, 8, 7, 7) for _ in range(2)],
             dma,
             dma,
         ],

time: 25.4 us -> 25.2 us (level)
  no operation moved by 1% of the time
where the time goes in v6:
time: 25.2 us; the launch traced here: 25 us
  Pallas kernels  24.4 us (97%)
  between operations  0.64 us (3%)
    pallas_call x1, Pallas kernels, body(): pl.pallas_call(kernel, out_shape=(pltpu.VMEM(ensemble.shape, BF16), pltpu...  23.6 us
    pallas_call x1, Pallas kernels, body(): pl.pallas_call(written, out_shape=(jax.ShapeDtypeStruct(ensemble.shape, B...  0.81 us

profile of v6, /device:TPU:1, one launch (start us, length us, event | category | flops | bytes accessed | tf_op | source)
XLA Modules:
  0.0 25.0 jit_solution(9448185352524754382)
XLA Ops:
  0.6 23.6 %shard_map.86 = (bf16[10,16384]{1,0:T(8,128)(2,1)S(1)}, f32[1,16]{1,0:T(1,128)S(1)}) custom-call(bf16[10,16384]{1,0:T(8,128)(2,1)} %ens.1, f32[32,128]{1,0:T(8,128)} %val.1, f32[32,128]{1,0:T(8,128)} %var.1, s32[32,128]{1,0:T(8,128)} %pnt.1, s32[1,128]{1,0:T(1,128)} %bitcast.6, f32[32,128]{1,0:T(8,128)} %bitcast.4, f32[32,128]{1,0:T(8,128)} %bitcast.5), custom_call_target="tpu_custom_call" | custom-call | tf_op jit(solution)/shard_map/pallas_call | solution.py:402
  24.2 0.8 %shard_map.87 = (bf16[10,16384]{1,0:T(8,128)(2,1)}, f32[1,16]{1,0:T(1,128)}) custom-call(bf16[10,16384]{1,0:T(8,128)(2,1)S(1)} %get-tuple-element.6.a, f32[1,16]{1,0:T(1,128)S(1)} %get-tuple-element.7.b), custom_call_target="tpu_custom_call" | custom-call | tf_op jit(solution)/shard_map/pallas_call | solution.py:446

commit v7 on v6

--- a/solution.py
+++ b/solution.py
@@ -190,7 +190,6 @@
 
     pl.semaphore_wait(barrier, len(others) + len(along_x) + 4)
 
-    order = (1, 3, 0)
     def core_copy(k, d):
         return pltpu.make_async_remote_copy(
             src_ref=(sums, counts)[k].at[1 - core, ys[d]],
@@ -204,8 +203,9 @@
     def chip_copy(k, d, turn=0):
         i = 3 if turn else d - 1
         to = 1 - core if turn else core
+        direct = k == 1 and d == 2
         return pltpu.make_async_remote_copy(
-            src_ref=(sums, counts)[k].at[to, ys[2]] if d == 2 else (sums_to, counts_to)[k].at[d],
+            src_ref=counts.at[to, ys[2]] if direct else (sums_to, counts_to)[k].at[d],
             dst_ref=(sums_chip, counts_chip)[k].at[i],
             send_sem=chip_send.at[4 * k + i],
             recv_sem=chip_recv.at[4 * k + i],
@@ -213,31 +213,28 @@
             device_id_type=MESH,
         )
 
-    chip_copies = [(k, d, turn) for k in (1, 0) for d, turn in ((1, 0), (3, 0), (2, 0), (2, 1))]
-
-    def pass_on(k):
-        own, came, total = ((sums, sums_core, sums_to), (counts, counts_core, counts_to))[k]
-        for d in order:
-            core_copy(k, d).wait_recv()
-            total[d] = own[core, ys[d]] + came[d]
-            if d:
-                chip_copy(k, d).start()
-
-    for d in order:
-        core_copy(1, d).start()
+    chip_copies = [(1, 1, 0), (1, 3, 0), (0, 1, 0), (0, 3, 0), (1, 2, 0), (1, 2, 1), (0, 2, 0)]
+    core_copies = [(1, 1), (1, 3), (0, 2), (0, 1), (0, 3), (1, 0), (0, 0)]
+
     for turn in range(2):
         chip_copy(1, 2, turn).start()
+    for copy in core_copies:
+        if copy[0]:
+            core_copy(*copy).start()
     for peer in (*along_x, *along_z[3:5]):
         pl.semaphore_signal(line_sem, inc=1, device_id={"region": peer}, device_id_type=MESH)
     for load in loads[3:]:
         load.wait()
     point_sums(ens_v, sums)
-    for d in order:
-        core_copy(0, d).start()
-    for turn in range(2):
-        chip_copy(0, 2, turn).start()
-    pass_on(1)
-    pass_on(0)
+    for copy in core_copies:
+        if not copy[0]:
+            core_copy(*copy).start()
+    for k, d in core_copies:
+        own, came, total = ((sums, sums_core, sums_to), (counts, counts_core, counts_to))[k]
+        core_copy(k, d).wait_recv()
+        total[d] = own[core, ys[d]] + came[d]
+        if d:
+            chip_copy(k, d).start()
     pl.semaphore_wait(line_sem, len(along_x) + 2)
     for peer in along_z:
         pl.semaphore_signal(all_sem, inc=1, device_id={"region": peer}, device_id_type=MESH)
@@ -257,8 +254,8 @@
 
     def summed(total, came, k, size=OWN):
         at = slice(k * OWN, k * OWN + size)
-        near = total[0, at, :] + (came[0, at, :] + came[2, at, :])
-        return near + (came[1, at, :] + came[3, at, :])
+        terms = [came[i, at, :] for i in range(came.shape[0])]
+        return total[0, at, :] + sum(terms[1:], terms[0])
 
     mean = summed(sums_to, sums_chip, 0) / 80.0
     first = core * HALF + y * OWN
@@ -371,9 +368,8 @@
         device_id={"member": others[0]},
         device_id_type=MESH,
     )
-    for k in range(2):
-        for d in order:
-            core_copy(k, d).wait_send()
+    for copy in core_copies:
+        core_copy(*copy).wait_send()
     for copy in chip_copies:
         chip_copy(*copy).wait_send()
     for copy in (*mean_copies, *lam_copies, arrived):
@@ -417,9 +413,11 @@
             pltpu.VMEM((8, HALF), F32),
             *[
                 pltpu.VMEM((*lead, rows, LANES), F32)
-                for lead in ((2, 4), (4,), (4,), (4,))
+                for lead in ((2, 4), (4,), (4,))
                 for rows in (POINTS, COUNTS)
             ],
+            pltpu.VMEM((3, POINTS, LANES), F32),
+            pltpu.VMEM((4, COUNTS, LANES), F32),
             pltpu.VMEM((LANES, LANES), F32),
             pltpu.VMEM((1, LANES), F32),
             pltpu.VMEM((7, 1, LANES), F32),

time: 25.2 us -> 24.9 us (0.988)
  Pallas kernels: 24.4 us -> 24.1 us
    pallas_call x1, Pallas kernels: 23.6 us -> 23.3 us  [body(): pl.pallas_call(kernel, out_shape=(pltpu.VMEM(ensemble.shape, BF16), pltpu...]
where the time goes in v7:
time: 24.9 us; the launch traced here: 24.8 us
  Pallas kernels  24.1 us (97%)
  between operations  0.64 us (3%)
    pallas_call x1, Pallas kernels, body(): pl.pallas_call(kernel, out_shape=(pltpu.VMEM(ensemble.shape, BF16), pltpu...  23.3 us
    pallas_call x1, Pallas kernels, body(): pl.pallas_call(written, out_shape=(jax.ShapeDtypeStruct(ensemble.shape, B...  0.81 us

profile of v7, /device:TPU:1, one launch (start us, length us, event | category | flops | bytes accessed | tf_op | source)
XLA Modules:
  0.0 24.8 jit_solution(18023350821573961127)
XLA Ops:
  0.6 23.3 %shard_map.86 = (bf16[10,16384]{1,0:T(8,128)(2,1)S(1)}, f32[1,16]{1,0:T(1,128)S(1)}) custom-call(bf16[10,16384]{1,0:T(8,128)(2,1)} %ens.1, f32[32,128]{1,0:T(8,128)} %val.1, f32[32,128]{1,0:T(8,128)} %var.1, s32[32,128]{1,0:T(8,128)} %pnt.1, s32[1,128]{1,0:T(1,128)} %bitcast.6, f32[32,128]{1,0:T(8,128)} %bitcast.4, f32[32,128]{1,0:T(8,128)} %bitcast.5), custom_call_target="tpu_custom_call" | custom-call | tf_op jit(solution)/shard_map/pallas_call | solution.py:398
  23.9 0.8 %shard_map.87 = (bf16[10,16384]{1,0:T(8,128)(2,1)}, f32[1,16]{1,0:T(1,128)}) custom-call(bf16[10,16384]{1,0:T(8,128)(2,1)S(1)} %get-tuple-element.6.a, f32[1,16]{1,0:T(1,128)S(1)} %get-tuple-element.7.b), custom_call_target="tpu_custom_call" | custom-call | tf_op jit(solution)/shard_map/pallas_call | solution.py:444

commit v8 on v7

--- a/solution.py
+++ b/solution.py
@@ -13,7 +13,8 @@
 LANES = 128
 HALF = 64
 POINTS = 2 * OWN
-COUNTS = 3 * OWN + 8
+COUNTS = 3 * OWN + 2
+EARLY = 4
 STEP = 32
 
 
@@ -25,8 +26,8 @@
     return [p.astype(F32) for p in parts]
 
 
-def point_sums(ens_v, sums):
-    @pl.loop(0, 16)
+def point_sums(ens_v, sums, first, last):
+    @pl.loop(first, last)
     def _(j):
         x = ens_v[:, pl.ds(pl.multiple_of(j * 1024, 1024), 1024)].astype(F32)
         total = jnp.sum(x, axis=0, keepdims=True)
@@ -101,8 +102,13 @@
             acc[...] += more
             acc_q[...] += more_q
 
-    squares = jnp.concatenate([acc_q[:4, :], acc_q[4:, :]], axis=1)
-    squares = jnp.concatenate([squares, squares], axis=0)
+    squares = jnp.concatenate(
+        [
+            jnp.concatenate([acc_q[k : k + 1, :] + acc_q[k + 1 : k + 2, :] for k in (0, 2)], axis=0),
+            jnp.concatenate([acc_q[k : k + 1, :] + acc_q[k + 1 : k + 2, :] for k in (4, 6)], axis=0),
+        ],
+        axis=1,
+    )
     for parity in range(2):
         lanes = slice(parity * LANES, (parity + 1) * LANES)
         for y in range(4):
@@ -188,6 +194,9 @@
         load.wait()
     histograms(val_v, var_v, pnt_v, rows_v, acc, acc_q, counts)
 
+    for load in loads[3:]:
+        load.wait()
+    point_sums(ens_v, sums, 0, EARLY)
     pl.semaphore_wait(barrier, len(others) + len(along_x) + 4)
 
     def core_copy(k, d):
@@ -223,9 +232,7 @@
             core_copy(*copy).start()
     for peer in (*along_x, *along_z[3:5]):
         pl.semaphore_signal(line_sem, inc=1, device_id={"region": peer}, device_id_type=MESH)
-    for load in loads[3:]:
-        load.wait()
-    point_sums(ens_v, sums)
+    point_sums(ens_v, sums, EARLY, 16)
     for copy in core_copies:
         if not copy[0]:
             core_copy(*copy).start()
@@ -263,17 +270,17 @@
     means[my_rows, :] = mean
     spread = (summed(sums_to, sums_chip, 1) - 80.0 * mean * mean) / 79.0
     count, value, error = (summed(counts_to, counts_chip, k) for k in range(3))
-    squares = summed(counts_to, counts_chip, 3, 8)
+    squares = summed(counts_to, counts_chip, 3, 2)
     mine = lane == sub + first
 
     def per_slot(x):
         return jnp.sum(x, axis=1, keepdims=True)
 
     innov_sum = per_slot(
-        jnp.where(mine, jnp.sum(squares[0:2], axis=0, keepdims=True), 0.0)
+        jnp.where(mine, squares[0:1], 0.0)
         + mean * (count * mean - 2.0 * value)
     )
-    error_error = per_slot(jnp.where(mine, jnp.sum(squares[2:4], axis=0, keepdims=True), 0.0))
+    error_error = per_slot(jnp.where(mine, squares[1:2], 0.0))
     count_spread = count * spread
     spread_sum = per_slot(count_spread)
     spread_spread = per_slot(count_spread * spread)

time: 24.9 us -> 24.6 us (0.988)
  Pallas kernels: 24.1 us -> 23.8 us
    pallas_call x1, Pallas kernels: 23.3 us -> 23 us  [body(): pl.pallas_call(kernel, out_shape=(pltpu.VMEM(ensemble.shape, BF16), pltpu...]
where the time goes in v8:
time: 24.6 us; the launch traced here: 24.4 us
  Pallas kernels  23.8 us (97%)
  between operations  0.64 us (3%)
    pallas_call x1, Pallas kernels, body(): pl.pallas_call(kernel, out_shape=(pltpu.VMEM(ensemble.shape, BF16), pltpu...  23 us
    pallas_call x1, Pallas kernels, body(): pl.pallas_call(written, out_shape=(jax.ShapeDtypeStruct(ensemble.shape, B...  0.81 us

profile of v8, /device:TPU:1, one launch (start us, length us, event | category | flops | bytes accessed | tf_op | source)
XLA Modules:
  0.0 24.4 jit_solution(11668766172086599004)
XLA Ops:
  0.6 23.0 %shard_map.86 = (bf16[10,16384]{1,0:T(8,128)(2,1)S(1)}, f32[1,16]{1,0:T(1,128)S(1)}) custom-call(bf16[10,16384]{1,0:T(8,128)(2,1)} %ens.1, f32[32,128]{1,0:T(8,128)} %val.1, f32[32,128]{1,0:T(8,128)} %var.1, s32[32,128]{1,0:T(8,128)} %pnt.1, s32[1,128]{1,0:T(1,128)} %bitcast.6, f32[32,128]{1,0:T(8,128)} %bitcast.4, f32[32,128]{1,0:T(8,128)} %bitcast.5), custom_call_target="tpu_custom_call" | custom-call | tf_op jit(solution)/shard_map/pallas_call | solution.py:405
  23.6 0.8 %shard_map.87 = (bf16[10,16384]{1,0:T(8,128)(2,1)}, f32[1,16]{1,0:T(1,128)}) custom-call(bf16[10,16384]{1,0:T(8,128)(2,1)S(1)} %get-tuple-element.6.a, f32[1,16]{1,0:T(1,128)S(1)} %get-tuple-element.7.b), custom_call_target="tpu_custom_call" | custom-call | tf_op jit(solution)/shard_map/pallas_call | solution.py:451

commit v9 on v8

--- a/solution.py
+++ b/solution.py
@@ -330,6 +330,7 @@
             )
         )
         lam_copies[-1].start()
+    to_all(everyone[96:])
     mean_copies = []
     for i, peer in enumerate(others):
         mean_copies.append(
@@ -344,7 +345,6 @@
         )
         mean_copies[-1].start()
 
-    to_all(everyone[96:])
     for copy in lam_copies:
         copy.wait_recv()
     lam_row = my_lam[...]

time: 24.6 us -> 24.6 us (level)
  no operation moved by 1% of the time
where the time goes in v9:
time: 24.6 us; the launch traced here: 24.4 us
  Pallas kernels  23.7 us (96%)
  between operations  0.64 us (3%)
    pallas_call x1, Pallas kernels, body(): pl.pallas_call(kernel, out_shape=(pltpu.VMEM(ensemble.shape, BF16), pltpu...  22.9 us
    pallas_call x1, Pallas kernels, body(): pl.pallas_call(written, out_shape=(jax.ShapeDtypeStruct(ensemble.shape, B...  0.81 us

profile of v9, /device:TPU:1, one launch (start us, length us, event | category | flops | bytes accessed | tf_op | source)
XLA Modules:
  0.0 24.4 jit_solution(4710057400233550185)
XLA Ops:
  0.6 22.9 %shard_map.86 = (bf16[10,16384]{1,0:T(8,128)(2,1)S(1)}, f32[1,16]{1,0:T(1,128)S(1)}) custom-call(bf16[10,16384]{1,0:T(8,128)(2,1)} %ens.1, f32[32,128]{1,0:T(8,128)} %val.1, f32[32,128]{1,0:T(8,128)} %var.1, s32[32,128]{1,0:T(8,128)} %pnt.1, s32[1,128]{1,0:T(1,128)} %bitcast.6, f32[32,128]{1,0:T(8,128)} %bitcast.4, f32[32,128]{1,0:T(8,128)} %bitcast.5), custom_call_target="tpu_custom_call" | custom-call | tf_op jit(solution)/shard_map/pallas_call | solution.py:405
  23.6 0.8 %shard_map.87 = (bf16[10,16384]{1,0:T(8,128)(2,1)}, f32[1,16]{1,0:T(1,128)}) custom-call(bf16[10,16384]{1,0:T(8,128)(2,1)S(1)} %get-tuple-element.6.a, f32[1,16]{1,0:T(1,128)S(1)} %get-tuple-element.7.b), custom_call_target="tpu_custom_call" | custom-call | tf_op jit(solution)/shard_map/pallas_call | solution.py:451

commit v10 on v9

--- a/solution.py
+++ b/solution.py
@@ -164,14 +164,26 @@
     from_region[255:256, :] = jnp.zeros((1, LANES), F32)
 
     region, member = lax.axis_index("region"), lax.axis_index("member")
+    barrier = pltpu.get_barrier_semaphore()
+
+    def greet(**peer):
+        pl.semaphore_signal(barrier, inc=1, device_id=peer, device_id_type=MESH)
+
+    x, z = lax.div(region, 8), lax.rem(region, 8)
+    zs = [z, *(lax.rem(z + d, 8) for d in range(1, 8))]
+    along_z = [8 * x + zs[d] for d in (4, 3, 5, 2, 6, 1, 7)]
+    for peer in along_z[3:5]:
+        greet(region=peer)
+    xs = [8 * x, *(8 * lax.rem(x + d, 4) for d in range(1, 4))]
+    along_x = [xs[d] + z for d in (2, 1, 3)]
+    greet(region=along_x[0])
     y, core = lax.div(member, 2), lax.rem(member, 2)
     ys = [y, *(lax.rem(y + d, 4) for d in range(1, 4))]
     others = [2 * ys[d] + c for d in (2, 1, 3) for c in (core, 1 - core)] + [2 * y + 1 - core]
-    x, z = lax.div(region, 8), lax.rem(region, 8)
-    xs = [8 * lax.rem(x + d, 4) for d in range(4)]
-    zs = [lax.rem(z + d, 8) for d in range(8)]
-    along_x = [xs[d] + zs[0] for d in (2, 1, 3)]
-    along_z = [xs[0] + zs[d] for d in (4, 3, 5, 2, 6, 1, 7)]
+    for peer in others:
+        greet(member=peer)
+    for peer in (*along_x[1:], *along_z[5:]):
+        greet(region=peer)
     members = [2 * ys[d] + c for d in range(4) for c in (core, 1 - core)]
     apart = sorted(
         (
@@ -181,14 +193,6 @@
         )
     )
     peers = [(xs[dx] + zs[dz], members[2 * dy + c]) for _, (dx, dz, dy, c) in apart]
-
-    barrier = pltpu.get_barrier_semaphore()
-    for peer in (along_x[0], *along_z[3:5]):
-        pl.semaphore_signal(barrier, inc=1, device_id={"region": peer}, device_id_type=MESH)
-    for peer in others:
-        pl.semaphore_signal(barrier, inc=1, device_id={"member": peer}, device_id_type=MESH)
-    for peer in (*along_x[1:], *along_z[5:]):
-        pl.semaphore_signal(barrier, inc=1, device_id={"region": peer}, device_id_type=MESH)
 
     for load in loads[:3]:
         load.wait()

time: 24.6 us -> 24.5 us (level)
  no operation moved by 1% of the time
where the time goes in v10:
time: 24.5 us; the launch traced here: 24.4 us
  Pallas kernels  23.7 us (97%)
  between operations  0.64 us (3%)
    pallas_call x1, Pallas kernels, body(): pl.pallas_call(kernel, out_shape=(pltpu.VMEM(ensemble.shape, BF16), pltpu...  22.9 us
    pallas_call x1, Pallas kernels, body(): pl.pallas_call(written, out_shape=(jax.ShapeDtypeStruct(ensemble.shape, B...  0.81 us

profile of v10, /device:TPU:1, one launch (start us, length us, event | category | flops | bytes accessed | tf_op | source)
XLA Modules:
  0.0 24.4 jit_solution(10116369209415108193)
XLA Ops:
  0.6 22.9 %shard_map.86 = (bf16[10,16384]{1,0:T(8,128)(2,1)S(1)}, f32[1,16]{1,0:T(1,128)S(1)}) custom-call(bf16[10,16384]{1,0:T(8,128)(2,1)} %ens.1, f32[32,128]{1,0:T(8,128)} %val.1, f32[32,128]{1,0:T(8,128)} %var.1, s32[32,128]{1,0:T(8,128)} %pnt.1, s32[1,128]{1,0:T(1,128)} %bitcast.6, f32[32,128]{1,0:T(8,128)} %bitcast.4, f32[32,128]{1,0:T(8,128)} %bitcast.5), custom_call_target="tpu_custom_call" | custom-call | tf_op jit(solution)/shard_map/pallas_call | solution.py:409
  23.5 0.8 %shard_map.87 = (bf16[10,16384]{1,0:T(8,128)(2,1)}, f32[1,16]{1,0:T(1,128)}) custom-call(bf16[10,16384]{1,0:T(8,128)(2,1)S(1)} %get-tuple-element.6.a, f32[1,16]{1,0:T(1,128)S(1)} %get-tuple-element.7.b), custom_call_target="tpu_custom_call" | custom-call | tf_op jit(solution)/shard_map/pallas_call | solution.py:455

commit v11 on v8

--- a/solution.py
+++ b/solution.py
@@ -264,11 +264,11 @@
         terms = [came[i, at, :] for i in range(came.shape[0])]
         return total[0, at, :] + sum(terms[1:], terms[0])
 
-    mean = summed(sums_to, sums_chip, 0) / 80.0
+    mean = summed(sums_to, sums_chip, 0) * (1.0 / 80.0)
     first = core * HALF + y * OWN
     my_rows = pl.ds(pl.multiple_of(first, OWN), OWN)
     means[my_rows, :] = mean
-    spread = (summed(sums_to, sums_chip, 1) - 80.0 * mean * mean) / 79.0
+    spread = (summed(sums_to, sums_chip, 1) - 80.0 * mean * mean) * (1.0 / 79.0)
     count, value, error = (summed(counts_to, counts_chip, k) for k in range(3))
     squares = summed(counts_to, counts_chip, 3, 2)
     mine = lane == sub + first

time: 24.6 us -> 24.6 us (level)
  no operation moved by 1% of the time
where the time goes in v11:
time: 24.6 us; the launch traced here: 24.4 us
  Pallas kernels  23.8 us (97%)
  between operations  0.64 us (3%)
    pallas_call x1, Pallas kernels, body(): pl.pallas_call(kernel, out_shape=(pltpu.VMEM(ensemble.shape, BF16), pltpu...  23 us
    pallas_call x1, Pallas kernels, body(): pl.pallas_call(written, out_shape=(jax.ShapeDtypeStruct(ensemble.shape, B...  0.81 us

profile of v11, /device:TPU:1, one launch (start us, length us, event | category | flops | bytes accessed | tf_op | source)
XLA Modules:
  0.0 24.4 jit_solution(11668766172086599004)
XLA Ops:
  0.6 23.0 %shard_map.86 = (bf16[10,16384]{1,0:T(8,128)(2,1)S(1)}, f32[1,16]{1,0:T(1,128)S(1)}) custom-call(bf16[10,16384]{1,0:T(8,128)(2,1)} %ens.1, f32[32,128]{1,0:T(8,128)} %val.1, f32[32,128]{1,0:T(8,128)} %var.1, s32[32,128]{1,0:T(8,128)} %pnt.1, s32[1,128]{1,0:T(1,128)} %bitcast.6, f32[32,128]{1,0:T(8,128)} %bitcast.4, f32[32,128]{1,0:T(8,128)} %bitcast.5), custom_call_target="tpu_custom_call" | custom-call | tf_op jit(solution)/shard_map/pallas_call | solution.py:405
  23.6 0.8 %shard_map.87 = (bf16[10,16384]{1,0:T(8,128)(2,1)}, f32[1,16]{1,0:T(1,128)}) custom-call(bf16[10,16384]{1,0:T(8,128)(2,1)S(1)} %get-tuple-element.6.a, f32[1,16]{1,0:T(1,128)S(1)} %get-tuple-element.7.b), custom_call_target="tpu_custom_call" | custom-call | tf_op jit(solution)/shard_map/pallas_call | solution.py:451
